TPU v7x, 512 devices: a whole 4x8x8 slice. The times are simulated.
512 devices in a mesh: dp: 8 (over y_hi, core), tensor: 64 (over x, z, y_lo).
Axes of the slice: x: 4, y: 8 (y_hi: 4, y_lo: 2; y = y_hi * 2 + y_lo), z: 8, core: 2. Of those that a mesh axis runs over, the one named last changes fastest.
Arguments:
- gradient: float32 [8, 8192, 512], P('dp', 'tensor'), may hold values from -80 to 80
Outputs:
- update: bfloat16 [8, 8192, 512], P(None, 'tensor')
All inputs are finite; a program needn't handle non-finite values.
Results may differ from a plain program's by a relative error of at most 0.001.
Values may be sent and summed in bfloat16 or wider, within the bound.
A program may use at most 64 MiB of HBM per device.

v0:
```python
import math

import jax
import jax.numpy as jnp
from jax import lax
from jax.sharding import PartitionSpec as P

FEATURES = 8192
OUTPUTS = 512
ITERS = 3


linear_term = 3.4445
cubic_term = -4.775
quintic_term = 2.0315
norm_floor = 1e-07
update_gain = 0.2


def rows_for(lines, size):
    spare = -len(lines) % size
    return jnp.pad(lines, [(0, spare)] + [(0, 0)] * (lines.ndim - 1))


def in_order(tiles, dim):
    lengths = list(tiles.shape[1:])
    lengths[dim] *= tiles.shape[0]
    return jnp.moveaxis(tiles, 0, dim).reshape(lengths)


def from_everyone(shard, axis):
    size = lax.axis_size(axis)
    return lax.all_to_all(
        jnp.broadcast_to(shard[None], (size, *shard.shape)), axis, 0, 0, tiled=True
    )


def gather_directly(shard, axis, dim):
    return in_order(from_everyone(shard, axis), dim)


def split_up(shard, dim, size):
    before, after = (shard.shape[:dim], shard.shape[dim + 1 :])
    return jnp.moveaxis(shard.reshape(*before, size, -1, *after), dim, 0)


def summed_on_arrival(shard, axis, dim):
    tiles = split_up(shard, dim, lax.axis_size(axis))
    arrived = lax.all_to_all(tiles, axis, split_axis=0, concat_axis=0, tiled=True)
    return arrived.sum(axis=0)


def sum_by_parts(shard, axes):
    lines = shard.reshape(-1, shard.shape[-1])
    padded = rows_for(lines, lax.axis_size(axes))
    whole = gather_directly(summed_on_arrival(padded, axes, 0), axes, 0)
    return lax.slice_in_dim(whole, 0, len(lines)).reshape(shard.shape)


def multiply(first_factor, second_factor):
    return jnp.einsum("mrs,mst->mrt", first_factor, second_factor, precision=lax.Precision.HIGHEST)


def block_pairs():
    return [
        (left_block, right_block) for left_block in range(4) for right_block in range(left_block, 4)
    ]


def local_gram(gradient):
    quarter = gradient.shape[2] // 4
    blocks = gradient.reshape(gradient.shape[0], gradient.shape[1], 4, quarter)
    products_list = [
        jnp.einsum(
            "mfr,mfs->mrs",
            blocks[:, :, left_block],
            blocks[:, :, right_block],
            precision=lax.Precision.HIGHEST,
        )
        for left_block, right_block in block_pairs()
    ]
    return jnp.stack(products_list, axis=1)


def expand_gram(summed):
    position = {}
    for slot_index, block_pair in enumerate(block_pairs()):
        position[block_pair] = slot_index
    block_rows = []
    for left_block in range(4):
        row_blocks = []
        for right_block in range(4):
            if left_block <= right_block:
                row_blocks.append(summed[:, position[left_block, right_block]])
            else:
                row_blocks.append(jnp.swapaxes(summed[:, position[right_block, left_block]], 1, 2))
        block_rows.append(jnp.concatenate(row_blocks, axis=2))
    return jnp.concatenate(block_rows, axis=1)


def reduce_gram(partial_gram):
    return sum_by_parts(partial_gram, "tensor")


def replicated_total(gram_matrix):
    order = gram_matrix.shape[2]
    identity = jnp.eye(order, dtype=jnp.float32)[None]
    running = identity
    for turn_index in range(ITERS):
        squared = multiply(gram_matrix, gram_matrix)
        polynomial = linear_term * identity + cubic_term * gram_matrix + quintic_term * squared
        if turn_index == 0:
            running = polynomial
        else:
            running = multiply(running, polynomial)
        if turn_index + 1 < ITERS:
            gram_matrix = multiply(multiply(polynomial, gram_matrix), polynomial)
    return running


def on_device(gradient):
    summed = expand_gram(reduce_gram(local_gram(gradient)))
    squared_norm = jnp.sum(jnp.diagonal(summed, axis1=1, axis2=2), axis=1)
    divisor = jnp.sqrt(squared_norm) + norm_floor
    gram_matrix = summed / (divisor * divisor)[:, None, None]
    polished = jnp.einsum(
        "mfr,mrs->mfs", gradient, replicated_total(gram_matrix), precision=lax.Precision.HIGHEST
    )
    factor = update_gain * math.sqrt(max(FEATURES, OUTPUTS)) / divisor
    update = (factor[:, None, None] * polished).astype(jnp.bfloat16)
    return gather_directly(update, "dp", 0)


def solution(mesh):
    placed = (P("dp", "tensor", None),)
    return jax.shard_map(
        on_device, mesh=mesh, in_specs=placed, out_specs=P(None, "tensor", None), check_vma=False
    )
```

profile of v0, /device:TPU:6, one launch (start us, length us, event | category | flops | bytes accessed | tf_op | source)
XLA Modules:
  0.0 133.9 jit_solution(17316398745980531288)
XLA Ops:
  0.0 1.0 reshape.191
  1.8 0.3 fusion.12
  2.1 0.3 fusion.11
  2.4 0.3 fusion.10
  2.7 0.3 fusion.9
  3.0 0.3 fusion.8
  4.2 36.4 %all_to_all.15 = f32[64,20,128]{2,1,0:T(8,128)S(1)} all-to-all(f32[64,20,128]{2,1,0:T(8,128)S(1)} %reshape.196), channel_id=1, replica_groups=mesh['dp'=8,'tensor'=64] {'tensor'}, dimensions={0} | all-to-all | bytes 1310720 | tf_op jit(solution)/shard_map/all_to_all | solution.py:49
  40.7 0.9 broadcast_in_dim.8
  41.6 7.8 %all-to-all-start.1 = ((f32[64,20,128]{2,1,0:T(8,128)}), f32[64,20,128]{2,1,0:T(8,128)S(1)}, u32[]{:S(2)}, u32[]{:S(2)}) async-start(f32[64,20,128]{2,1,0:T(8,128)} %broadcast_in_dim.8), calls=%async_computation.1 | async-start | bytes 1572864 | tf_op jit(solution)/shard_map/all_to_all | solution.py:33
  49.4 21.5 %all-to-all-done.1 = f32[64,20,128]{2,1,0:T(8,128)S(1)} async-done(((f32[64,20,128]{2,1,0:T(8,128)}), f32[64,20,128]{2,1,0:T(8,128)S(1)}, u32[]{:S(2)}, u32[]{:S(2)}) %all-to-all-start.1) | async-done | bytes 655392 | tf_op jit(solution)/shard_map/all_to_all | solution.py:33
  72.1 4.7 %gather_fusion = f32[512]{0:T(512)S(1)} fusion(f32[512,512]{1,0:T(8,128)S(1)} %maximum_bitcast_fusion, s32[512]{0:T(512)S(1)} %bitcast.132), kind=kCustom, calls=%fused_computation | custom fusion | bytes 8192 | tf_op jit(solution)/shard_map/jit(diagonal)/gather | solution.py:123
  76.9 0.6 reduce.1
  78.1 2.0 %fusion.2 = f32[512,512]{1,0:T(8,128)S(1)} fusion(f32[]{:T(128)S(6)} %mul.50, f32[128,512]{1,0:T(8,128)S(1)} %maximum_bitcast_fusion.3, f32[128,512]{1,0:T(8,128)S(1)} %get-tuple-element.26, f32[128,512]{1,0:T(8,128)S(1)} %copy.28, f32[128,512]{1,0:T(8,128)S(1)} %get-tuple-element.25), kind=kOutput, calls=%fused_computation.9 | convolution fusion | flops 1614282752 | bytes 2097156 | tf_op jit(solution)/shard_map/mrs,mst->mrt/dot_general | solution.py:61
  80.2 1.9 %fusion.16 = f32[512,512]{1,0:T(8,128)S(1)} fusion(f32[512,512]{1,0:T(8,128)S(1)} %fusion.2, f32[128,512]{1,0:T(8,128)S(1)} %maximum_bitcast_fusion.3, f32[128,512]{1,0:T(8,128)S(1)} %get-tuple-element.26, f32[128,512]{1,0:T(8,128)S(1)} %copy.28, f32[128,512]{1,0:T(8,128)S(1)} %get-tuple-element.25, f32[]{:T(128)S(6)} %mul.50), kind=kOutput, calls=%fused_computation.53 | convolution fusion | flops 1611661312 | bytes 3145732 | tf_op jit(solution)/shard_map/mrs,mst->mrt/dot_general | solution.py:61
  82.0 1.9 %fusion.19 = f32[512,512]{1,0:T(8,128)S(1)} fusion(f32[512,512]{1,0:T(8,128)S(1)} %fusion.16, f32[512,512]{1,0:T(8,128)S(1)} %fusion.2), kind=kOutput, calls=%fused_computation.56 | convolution fusion | flops 1610612736 | bytes 3145728 | tf_op jit(solution)/shard_map/mrs,mst->mrt/dot_general | solution.py:61
  83.9 1.9 %fusion.1 = f32[512,512]{1,0:T(8,128)S(1)} fusion(f32[512,512]{1,0:T(8,128)S(1)} %fusion.19), kind=kOutput, calls=%fused_computation.7 | convolution fusion | flops 1612185600 | bytes 2097152 | tf_op jit(solution)/shard_map/mrs,mst->mrt/dot_general | solution.py:61
  85.8 1.8 %fusion.21 = f32[512,512]{1,0:T(8,128)S(1)} fusion(f32[512,512]{1,0:T(8,128)S(1)} %fusion.1, f32[512,512]{1,0:T(8,128)S(1)} %fusion.19), kind=kOutput, calls=%fused_computation.58 | convolution fusion | flops 1610612736 | bytes 3145728 | tf_op jit(solution)/shard_map/mrs,mst->mrt/dot_general | solution.py:61
  87.6 1.9 %fusion.20 = f32[512,512]{1,0:T(8,128)S(1)} fusion(f32[512,512]{1,0:T(8,128)S(1)} %fusion.2, f32[512,512]{1,0:T(8,128)S(1)} %fusion.1), kind=kOutput, calls=%fused_computation.57 | convolution fusion | flops 1610612736 | bytes 3145728 | tf_op jit(solution)/shard_map/mrs,mst->mrt/dot_general | solution.py:61
  89.6 1.8 %fusion.22 = f32[512,512]{1,0:T(8,128)S(1)} fusion(f32[512,512]{1,0:T(8,128)S(1)} %fusion.21, f32[512,512]{1,0:T(8,128)S(1)} %fusion.1), kind=kOutput, calls=%fused_computation.59 | convolution fusion | flops 1610612736 | bytes 3145728 | tf_op jit(solution)/shard_map/mrs,mst->mrt/dot_general | solution.py:61
  91.4 2.1 %fusion = f32[512,512]{1,0:T(8,128)S(1)} fusion(f32[512,512]{1,0:T(8,128)S(1)} %fusion.22), kind=kOutput, calls=%fused_computation.5 | convolution fusion | flops 1612185600 | bytes 2097152 | tf_op jit(solution)/shard_map/mrs,mst->mrt/dot_general | solution.py:61
  93.5 1.8 %fusion.23 = f32[512,512]{1,0:T(8,128)S(1)} fusion(f32[512,512]{1,0:T(8,128)S(1)} %fusion.20, f32[512,512]{1,0:T(8,128)S(1)} %fusion), kind=kOutput, calls=%fused_computation.60 | convolution fusion | flops 1610612736 | bytes 3145728 | tf_op jit(solution)/shard_map/mrs,mst->mrt/dot_general | solution.py:61
  95.4 1.8 %fusion.4 = bf16[128,512]{0,1:T(8,128)(2,1)S(1)} fusion(f32[512,512]{1,0:T(8,128)S(1)} %fusion.23, f32[1,128,512]{2,1,0:T(8,128)S(1)} %copy-done, f32[]{:T(128)S(6)} %div.17), kind=kOutput, calls=%fused_computation.12 | convolution fusion | flops 402784256 | bytes 1441796 | tf_op jit(solution)/shard_map/mfr,mrs->mfs/dot_general | solution.py:126
  97.4 35.5 %all_to_all.16 = bf16[8,1,128,512]{3,2,1,0:T(8,128)(2,1)S(1)} all-to-all(bf16[8,1,128,512]{3,2,1,0:T(8,128)(2,1)S(1)} %broadcast_in_dim.9), channel_id=1, replica_groups=mesh['dp'=8,'tensor'=64] {'dp'}, dimensions={0} | all-to-all | bytes 2097152 | tf_op jit(solution)/shard_map/all_to_all | solution.py:33
  132.9 1.0 copy.43
  (27 shorter events, 3.1 us)
Async XLA Ops:
  41.6 29.3 %all-to-all-start.1 = ((f32[64,20,128]{2,1,0:T(8,128)}), f32[64,20,128]{2,1,0:T(8,128)S(1)}, u32[]{:S(2)}, u32[]{:S(2)}) async-start(f32[64,20,128]{2,1,0:T(8,128)} %broadcast_in_dim.8), calls=%async_computation.1 | async-start | bytes 1572864 | tf_op jit(solution)/shard_map/all_to_all | solution.py:33
  93.5 1.9 %copy-start = (f32[1,128,512]{2,1,0:T(8,128)S(1)}, f32[1,128,512]{2,1,0:T(8,128)}, u32[]{:S(2)}) copy-start(f32[1,128,512]{2,1,0:T(8,128)} %param.1) | copy-start | bytes 786436
where the time goes:
time: 134 us
  blocking collectives  71.9 us (54%)
  matrix products  21.8 us (16%)
  waiting for transfers between devices  21.5 us (16%)
  local copies, waits for them, and re-layouts  9.02 us (7%)
  starting transfers between devices  7.77 us (6%)
    all_to_all x1, blocking collectives, summed_on_arrival(): lax.all_to_all(tiles, axis, split_axis=0, concat_axis=0, tiled=True)  36.4 us
    all_to_all x1, blocking collectives, from_everyone(): lax.all_to_all(jnp.broadcast_to(shard[None], (size, *shard.shape)), axis,...  35.5 us
    all_to_all x1, waiting for transfers between devices, from_everyone(): lax.all_to_all(jnp.broadcast_to(shard[None], (size, *shard.shape)), axis,...  21.5 us
    dot_general x9, matrix products, multiply(): jnp.einsum('mrs,mst->mrt', first_factor, second_factor, precision=lax.Pre...  17.1 us
    all_to_all x1, starting transfers between devices, from_everyone(): lax.all_to_all(jnp.broadcast_to(shard[None], (size, *shard.shape)), axis,...  7.77 us
    gather x1, local copies, waits for them, and re-layouts, on_device(): squared_norm = jnp.sum(jnp.diagonal(summed, axis1=1, axis2=2), axis=1)  4.7 us
    dot_general x10, matrix products, local_gram(): jnp.einsum('mfr,mfs->mrs', blocks[:, :, left_block], blocks[:, :, right_b...  2.84 us
  transfers between devices with their start and end apart: 1, of which 1 were waited for; matrix products, arithmetic and copies ran while one was open for 0% of the time, Pallas kernels for 0%

commit v1 on v0

v1 whole, which is shorter than its diff:
```python
import math

import jax
import jax.numpy as jnp
from jax import lax
from jax.experimental import pallas as pl
from jax.experimental.pallas import tpu as pltpu
from jax.sharding import PartitionSpec as P

FEATURES = 8192
OUTPUTS = 512

linear_term = 3.4445
cubic_term = -4.775
quintic_term = 2.0315
norm_floor = 1e-07
update_gain = 0.2

NX, NZ, NY = 4, 8, 2
PLANE = NX * NY
HI = 4
B = 128
STRIP = B // NZ
MESH = pl.DeviceIdType.MESH

f32 = jnp.float32
bf16 = jnp.bfloat16

OFF = [(0, 1), (0, 2), (0, 3), (1, 2), (1, 3), (2, 3)]


def halves(value):
    high = value.astype(bf16)
    low = (value - high.astype(f32)).astype(bf16)
    return high, low


def mm(a, b):
    return jnp.dot(a, b, preferred_element_type=f32)


def product(a, b):
    (ah, al), (bh, bl) = a, b
    return mm(ah, bh) + (mm(ah, bl) + mm(al, bh))


def kernel(x_ref, o_ref, pk, r1, st, r2, gf, g_ref,
           s1, v1, s2, v2, s3, v3, s4, v4, s5, v5):
    dp = lax.axis_index("dp")
    t = lax.axis_index("tensor")
    yl = lax.rem(t, NY)
    z = lax.rem(lax.div(t, NY), NZ)
    xx = lax.div(t, NY * NZ)
    hi = lax.div(dp, 2)
    core = lax.rem(dp, 2)
    q = xx * NY + yl

    def plane_peer(k):
        px = lax.rem(xx + k // NY, NX)
        py = lax.rem(yl + k % NY, NY)
        return px * NY + py, {"tensor": (px * NZ + z) * NY + py}

    def column_peer(k):
        pz = lax.rem(z + k, NZ)
        return pz, {"tensor": (xx * NZ + pz) * NY + yl}

    plane = [plane_peer(k) for k in range(1, PLANE)]
    column = [column_peer(k) for k in range(1, NZ)]
    d_right = lax.rem(hi + 1, HI) * 2 + core
    d_left = lax.rem(hi + HI - 1, HI) * 2 + core
    d_far = lax.rem(hi + 2, HI) * 2 + core
    mate = {"dp": hi * 2 + 1 - core}
    right = {"dp": d_right}
    left = {"dp": d_left}

    barrier = pltpu.get_barrier_semaphore()
    peers = [p for _, p in plane] + [p for _, p in column] + [right, left, mate]
    for peer in peers:
        pl.semaphore_signal(barrier, inc=1, device_id=peer, device_id_type=MESH)

    x = x_ref[0]
    xh, xl = halves(x)
    xth, xtl = halves(x.T)
    row = lax.broadcasted_iota(jnp.int32, (B, B), 0)
    col = lax.broadcasted_iota(jnp.int32, (B, B), 1)
    rows = []
    for i in range(4):
        a, b = i * B, (i + 1) * B
        rows.append(
            mm(xth[a:b], xh[:, a:]) + (mm(xth[a:b], xl[:, a:]) + mm(xtl[a:b], xh[:, a:]))
        )

    def block(i, j):
        return rows[i][:, (j - i) * B:(j - i + 1) * B]

    d1 = jnp.sum(jnp.where(row == col, block(1, 1), 0.0), axis=0, keepdims=True)
    d3 = jnp.sum(jnp.where(row == col, block(3, 3), 0.0), axis=0, keepdims=True)
    extra = jnp.concatenate([d1, d3, jnp.zeros((6, B), f32)], axis=0)
    pk[0, :B] = jnp.where(col >= row, block(0, 0), block(1, 1))
    pk[1, :B] = jnp.where(col >= row, block(2, 2), block(3, 3))
    for n, (i, j) in enumerate(OFF):
        pk[2 + n, :B] = block(i, j)
    for n in range(8):
        pk[n, B:] = extra

    pl.semaphore_wait(barrier, len(peers))

    def remote(src, dst, send, recv, peer):
        copy = pltpu.make_async_remote_copy(
            src_ref=src, dst_ref=dst, send_sem=send, recv_sem=recv,
            device_id=peer, device_id_type=MESH,
        )
        copy.start()
        return copy

    c1 = [
        remote(pk.at[pq], r1.at[k], s1.at[k], v1.at[k], peer)
        for k, (pq, peer) in enumerate(plane)
    ]
    for c in c1:
        c.wait_recv()
    acc = pk[q]
    for k in range(PLANE - 1):
        acc = acc + r1[k]
    for s in range(NZ):
        st[s, :STRIP] = acc[s * STRIP:(s + 1) * STRIP]
        st[s, STRIP:] = acc[B:]

    c2 = [
        remote(st.at[pz], r2.at[k], s2.at[k], v2.at[k], peer)
        for k, (pz, peer) in enumerate(column)
    ]
    for c in c2:
        c.wait_recv()
    acc = st[z]
    for k in range(NZ - 1):
        acc = acc + r2[k]
    gf[q, z] = acc[:STRIP]
    extra = acc[STRIP:]

    c3 = [
        remote(gf.at[q, z], gf.at[q, z], s3.at[k], v3.at[k], peer)
        for k, (_, peer) in enumerate(column)
    ]
    for c in c3:
        c.wait_recv()
    c4 = [
        remote(gf.at[q], gf.at[q], s4.at[k], v4.at[k], peer)
        for k, (_, peer) in enumerate(plane)
    ]
    for c in c4:
        c.wait_recv()

    def packed(n):
        return gf[n].reshape(B, B)

    diag = []
    trace = jnp.sum(extra[0:2], keepdims=True)
    for n in range(2):
        here = packed(n)
        flip = here.T
        upper = jnp.where(col >= row, here, flip)
        lower = jnp.where(
            row == col, jnp.broadcast_to(extra[n:n + 1], (B, B)), jnp.where(col < row, here, flip)
        )
        trace = trace + jnp.sum(jnp.where(row == col, here, 0.0), keepdims=True)
        diag += [upper, lower]
    divisor = jnp.sqrt(trace) + norm_floor
    inverse = 1.0 / (divisor * divisor)
    factor = (update_gain * math.sqrt(max(FEATURES, OUTPUTS))) / divisor
    for i in range(4):
        g_ref[i * B:(i + 1) * B, i * B:(i + 1) * B] = diag[i] * inverse
    for n, (i, j) in enumerate(OFF):
        here = packed(2 + n) * inverse
        g_ref[i * B:(i + 1) * B, j * B:(j + 1) * B] = here
        g_ref[j * B:(j + 1) * B, i * B:(i + 1) * B] = here.T

    identity = jnp.where(
        lax.broadcasted_iota(jnp.int32, (OUTPUTS, OUTPUTS), 0)
        == lax.broadcasted_iota(jnp.int32, (OUTPUTS, OUTPUTS), 1),
        linear_term,
        0.0,
    )
    gram = g_ref[...]
    tall = (xh, xl)
    for turn in range(2):
        pair = halves(gram)
        poly = halves(identity + cubic_term * gram + quintic_term * product(pair, pair))
        tall = halves(product(tall, poly))
        gram = product(pair, halves(product(poly, poly)))
    pair = halves(gram)
    base = tall[0].astype(f32) + tall[1].astype(f32)
    once = product(tall, pair)
    twice = product(halves(once), pair)
    polished = linear_term * base + cubic_term * once + quintic_term * twice
    o_ref[dp] = (factor * polished).astype(bf16)

    half = B // 2
    lo, up = pl.ds(0, half), pl.ds(half, half)
    n = iter(range(14))

    def send(matrix, part, peer):
        i = next(n)
        where = o_ref.at[matrix, part]
        return remote(where, where, s5.at[i], v5.at[i], peer)

    r_lo = send(dp, lo, right)
    l_up = send(dp, up, left)
    r_up = send(dp, up, right)
    l_lo = send(dp, lo, left)
    m_lo = send(dp, lo, mate)
    m_up = send(dp, up, mate)
    c5 = [r_lo, l_up, r_up, l_lo, m_lo, m_up]
    mates = [m_lo, m_up]
    r_lo.wait_recv()
    far_r = send(d_left, lo, right)
    l_up.wait_recv()
    far_l = send(d_right, up, left)
    more = [send(d_left, lo, mate), send(d_right, up, mate)]
    r_up.wait_recv()
    more.append(send(d_left, up, mate))
    l_lo.wait_recv()
    more.append(send(d_right, lo, mate))
    far_r.wait_recv()
    more.append(send(d_far, lo, mate))
    far_l.wait_recv()
    more.append(send(d_far, up, mate))
    mates += more
    c5 += [far_r, far_l] + more
    for c in mates:
        c.wait_recv()
    for c in c1 + c2 + c3 + c4 + c5:
        c.wait_send()


def on_device(gradient):
    dma = pltpu.SemaphoreType.DMA
    return pl.pallas_call(
        kernel,
        out_shape=jax.ShapeDtypeStruct((8, B, OUTPUTS), bf16),
        in_specs=[pl.BlockSpec(memory_space=pltpu.VMEM)],
        out_specs=pl.BlockSpec(memory_space=pltpu.VMEM),
        scratch_shapes=[
            pltpu.VMEM((8, B + 8, B), f32),
            pltpu.VMEM((PLANE - 1, B + 8, B), f32),
            pltpu.VMEM((NZ, STRIP + 8, B), f32),
            pltpu.VMEM((NZ - 1, STRIP + 8, B), f32),
            pltpu.VMEM((8, NZ, STRIP, B), f32),
            pltpu.VMEM((OUTPUTS, OUTPUTS), f32),
            dma((7,)), dma((7,)), dma((7,)), dma((7,)), dma((7,)),
            dma((7,)), dma((7,)), dma((7,)), dma((14,)), dma((14,)),
        ],
        compiler_params=pltpu.CompilerParams(collective_id=0, has_side_effects=True),
        name="gram_step",
    )(gradient)


def solution(mesh):
    return jax.shard_map(
        on_device,
        mesh=mesh,
        in_specs=(P("dp", "tensor", None),),
        out_specs=P(None, "tensor", None),
        check_vma=False,
    )
```

time: 134 us -> 61.5 us (0.46)
  the two profiles are of different devices: /device:TPU:6 before, /device:TPU:1 now
where the time goes in v1:
time: 61.5 us; the launch traced here: 61.3 us
  Pallas kernels  59.1 us (96%)
  local copies, waits for them, and re-layouts  2.26 us (4%)
    pallas_call x1, Pallas kernels, on_device(): pl.pallas_call(kernel, out_shape=jax.ShapeDtypeStruct((8, B, OUTPUTS), bf...  59.1 us
    unnamed x1, local copies, waits for them, and re-layouts  2.26 us

profile of v1, /device:TPU:1, one launch (start us, length us, event | category | flops | bytes accessed | tf_op | source)
XLA Modules:
  0.0 61.3 jit_solution(15320935255344110629)
XLA Ops:
  0.0 59.1 %gram_step.1 = bf16[8,128,512]{2,1,0:T(8,128)(2,1)} custom-call(f32[1,128,512]{2,1,0:T(8,128)} %x_ref.1), custom_call_target="tpu_custom_call" | custom-call | tf_op jit(solution)/shard_map/gram_step/pallas_call | solution.py:238
  59.1 2.3 %copy.3 = bf16[8,128,512]{2,1,0:T(8,128)(2,1)} copy(bf16[8,128,512]{2,1,0:T(8,128)(2,1)} %gram_step.1) | data formatting | bytes 2097152

commit v2 on v0

v2 whole, which is shorter than its diff:
```python
import math

import jax
import jax.numpy as jnp
from jax import lax
from jax.experimental import pallas as pl
from jax.experimental.pallas import tpu as pltpu
from jax.sharding import PartitionSpec as P

FEATURES = 8192
OUTPUTS = 512

linear_term = 3.4445
cubic_term = -4.775
quintic_term = 2.0315
norm_floor = 1e-07
update_gain = 0.2

NX, NZ, NY = 4, 8, 2
NEAR = NX * NY * 2
FAR = NZ // 2
HI = 4
B = 128
CHUNKS = 4
VMEM_LIMIT = 65850000
R = B // 2 // CHUNKS
MESH = pl.DeviceIdType.MESH

f32 = jnp.float32
bf16 = jnp.bfloat16

OFF = [(0, 1), (0, 2), (0, 3), (1, 2), (1, 3), (2, 3)]


def halves(value):
    high = value.astype(bf16)
    low = (value - high.astype(f32)).astype(bf16)
    return high, low


def mm(a, b):
    return jnp.dot(a, b, preferred_element_type=f32)


def product(a, b):
    (ah, al), (bh, bl) = a, b
    return mm(ah, bh) + (mm(ah, bl) + mm(al, bh))


def kernel(x_hbm, o_ref, x_ref, pk, r1, st, r2, gf, e_own, e1, e_near, e2, g_ref,
           x_sem, s1, v1, s2, v2, s3, v3, se, ve, s5, v5):
    dp = lax.axis_index("dp")
    t = lax.axis_index("tensor")
    yl = lax.rem(t, NY)
    z = lax.rem(lax.div(t, NY), NZ)
    zl = lax.rem(z, 2)
    zh = lax.div(z, 2)
    xx = lax.div(t, NY * NZ)
    hi = lax.div(dp, 2)
    core = lax.rem(dp, 2)
    me = (xx * NY + yl) * 2 + zl

    load = pltpu.make_async_copy(x_hbm.at[0], x_ref, x_sem)
    load.start()

    def near_peer(k):
        px = lax.rem(xx + k // 4, NX)
        py = lax.rem(yl + (k // 2) % 2, NY)
        pz = lax.rem(zl + k % 2, 2)
        return (px * NY + py) * 2 + pz, {"tensor": (px * NZ + zh * 2 + pz) * NY + py}

    def far_peer(k):
        return {"tensor": (xx * NZ + lax.rem(zh + k, FAR) * 2 + zl) * NY + yl}

    near = [near_peer(k) for k in range(1, NEAR)]
    far = [far_peer(k) for k in range(1, FAR)]
    d_right = lax.rem(hi + 1, HI) * 2 + core
    d_left = lax.rem(hi + HI - 1, HI) * 2 + core
    d_far = lax.rem(hi + 2, HI) * 2 + core
    mate = {"dp": hi * 2 + 1 - core}
    right = {"dp": d_right}
    left = {"dp": d_left}

    barrier = pltpu.get_barrier_semaphore()
    peers = [p for _, p in near] + far + [right, left, mate]
    for peer in peers:
        pl.semaphore_signal(barrier, inc=1, device_id=peer, device_id_type=MESH)
    load.wait()

    with jax.named_scope("gram_local"):
        x = x_ref[...]
        xh, xl = halves(x)
        xth, xtl = halves(x.T)
        row = lax.broadcasted_iota(jnp.int32, (B, B), 0)
        col = lax.broadcasted_iota(jnp.int32, (B, B), 1)
        rows = []
        for i in range(4):
            a, b = i * B, (i + 1) * B
            rows.append(
                mm(xth[a:b], xh[:, a:]) + (mm(xth[a:b], xl[:, a:]) + mm(xtl[a:b], xh[:, a:]))
            )

        def block(i, j):
            return rows[i][:, (j - i) * B:(j - i + 1) * B]

        def put(n, value):
            for h in range(2):
                for c in range(CHUNKS):
                    a = h * (B // 2) + c * R
                    pk[c, 2 * n + h] = value[a:a + R]

        put(0, jnp.where(col >= row, block(0, 0), block(1, 1)))
        put(1, jnp.where(col >= row, block(2, 2), block(3, 3)))
        for n, (i, j) in enumerate(OFF):
            put(2 + n, block(i, j))
        d1 = jnp.sum(jnp.where(row == col, block(1, 1), 0.0), axis=0, keepdims=True)
        d3 = jnp.sum(jnp.where(row == col, block(3, 3), 0.0), axis=0, keepdims=True)
        e_own[...] = jnp.concatenate([d1, d3], axis=0)

    with jax.named_scope("enter"):
        pl.semaphore_wait(barrier, len(peers))

    def remote(src, dst, send, recv, peer):
        copy = pltpu.make_async_remote_copy(
            src_ref=src, dst_ref=dst, send_sem=send, recv_sem=recv,
            device_id=peer, device_id_type=MESH,
        )
        copy.start()
        return copy

    def arrived(ref, sem):
        pltpu.make_async_remote_copy(
            src_ref=ref, dst_ref=ref, send_sem=sem, recv_sem=sem,
            device_id=mate, device_id_type=MESH,
        ).wait_recv()

    sent = []
    for c in range(CHUNKS):
        for k, (piece, peer) in enumerate(near):
            sent.append(remote(pk.at[c, piece], r1.at[c, k], s1.at[c], v1.at[c], peer))
    for k, (_, peer) in enumerate(near):
        sent.append(remote(e_own, e1.at[k], se.at[0], ve.at[0], peer))
    for c in range(CHUNKS):
        with jax.named_scope("near_sum"):
            arrived(r1.at[c], v1.at[c])
        acc = pk[c, me]
        for k in range(NEAR - 1):
            acc = acc + r1[c, k]
        st[c] = acc
        for k, peer in enumerate(far):
            sent.append(remote(st.at[c], r2.at[c, k], s2.at[c], v2.at[c], peer))
    arrived(e1, ve.at[0])
    extra = e_own[...]
    for k in range(NEAR - 1):
        extra = extra + e1[k]
    e_near[...] = extra
    for k, peer in enumerate(far):
        sent.append(remote(e_near, e2.at[k], se.at[1], ve.at[1], peer))
    for c in range(CHUNKS):
        with jax.named_scope("far_sum"):
            arrived(r2.at[c], v2.at[c])
        acc = st[c]
        for k in range(FAR - 1):
            acc = acc + r2[c, k]
        gf[c, me] = acc
        for k, (_, peer) in enumerate(near):
            sent.append(remote(gf.at[c, me], gf.at[c, me], s3.at[c], v3.at[c], peer))
    arrived(e2, ve.at[1])
    extra = e_near[...]
    for k in range(FAR - 1):
        extra = extra + e2[k]
    for c in range(CHUNKS):
        with jax.named_scope("gather"):
            arrived(gf.at[c, pl.ds(0, NEAR - 1)], v3.at[c])

    with jax.named_scope("expand"):
        def packed(n):
            return jnp.concatenate(
                [gf[c, 2 * n + h] for h in range(2) for c in range(CHUNKS)], axis=0
            )

        diag = []
        trace = jnp.sum(extra, keepdims=True)
        for n in range(2):
            here = packed(n)
            flip = here.T
            upper = jnp.where(col >= row, here, flip)
            lower = jnp.where(
                row == col, jnp.broadcast_to(extra[n:n + 1], (B, B)), jnp.where(col < row, here, flip)
            )
            trace = trace + jnp.sum(jnp.where(row == col, here, 0.0), keepdims=True)
            diag += [upper, lower]
        divisor = jnp.sqrt(trace) + norm_floor
        inverse = 1.0 / (divisor * divisor)
        factor = (update_gain * math.sqrt(max(FEATURES, OUTPUTS))) / divisor
        for i in range(4):
            g_ref[i * B:(i + 1) * B, i * B:(i + 1) * B] = diag[i] * inverse
        for n, (i, j) in enumerate(OFF):
            here = packed(2 + n) * inverse
            g_ref[i * B:(i + 1) * B, j * B:(j + 1) * B] = here
            g_ref[j * B:(j + 1) * B, i * B:(i + 1) * B] = here.T

    with jax.named_scope("chain"):
        identity = jnp.where(
            lax.broadcasted_iota(jnp.int32, (OUTPUTS, OUTPUTS), 0)
            == lax.broadcasted_iota(jnp.int32, (OUTPUTS, OUTPUTS), 1),
            linear_term,
            0.0,
        )
        gram = g_ref[...]
        tall = (xh, xl)
        for turn in range(2):
            pair = halves(gram)
            poly = halves(identity + cubic_term * gram + quintic_term * product(pair, pair))
            tall = halves(product(tall, poly))
            gram = product(pair, halves(product(poly, poly)))
        pair = halves(gram)
        base = tall[0].astype(f32) + tall[1].astype(f32)
        once = product(tall, pair)
        twice = product(halves(once), pair)
        polished = linear_term * base + cubic_term * once + quintic_term * twice
        o_ref[dp] = (factor * polished).astype(bf16)

    half = B // 2
    lo, up = pl.ds(0, half), pl.ds(half, half)
    n = iter(range(14))

    def send(matrix, part, peer):
        i = next(n)
        where = o_ref.at[matrix, part]
        copy = remote(where, where, s5.at[i], v5.at[i], peer)
        sent.append(copy)
        return copy

    with jax.named_scope("updates"):
        r_lo = send(dp, lo, right)
        l_up = send(dp, up, left)
        r_up = send(dp, up, right)
        l_lo = send(dp, lo, left)
        mates = [send(dp, lo, mate), send(dp, up, mate)]
        r_lo.wait_recv()
        far_r = send(d_left, lo, right)
        l_up.wait_recv()
        far_l = send(d_right, up, left)
        mates += [send(d_left, lo, mate), send(d_right, up, mate)]
        r_up.wait_recv()
        mates.append(send(d_left, up, mate))
        l_lo.wait_recv()
        mates.append(send(d_right, lo, mate))
        far_r.wait_recv()
        mates.append(send(d_far, lo, mate))
        far_l.wait_recv()
        mates.append(send(d_far, up, mate))
        for c in mates:
            c.wait_recv()
    for c in sent:
        c.wait_send()


def on_device(gradient):
    dma = pltpu.SemaphoreType.DMA
    updates = pl.pallas_call(
        kernel,
        out_shape=pltpu.VMEM((8, B, OUTPUTS), bf16),
        in_specs=[pl.BlockSpec(memory_space=pltpu.HBM)],
        out_specs=pl.BlockSpec(memory_space=pltpu.VMEM),
        scratch_shapes=[
            pltpu.VMEM((B, OUTPUTS), f32),
            pltpu.VMEM((CHUNKS, NEAR, R, B), f32),
            pltpu.VMEM((CHUNKS, NEAR - 1, R, B), f32),
            pltpu.VMEM((CHUNKS, R, B), f32),
            pltpu.VMEM((CHUNKS, FAR - 1, R, B), f32),
            pltpu.VMEM((CHUNKS, NEAR, R, B), f32),
            pltpu.VMEM((2, B), f32),
            pltpu.VMEM((NEAR - 1, 2, B), f32),
            pltpu.VMEM((2, B), f32),
            pltpu.VMEM((FAR - 1, 2, B), f32),
            pltpu.VMEM((OUTPUTS, OUTPUTS), f32),
            dma,
            dma((CHUNKS,)), dma((CHUNKS,)), dma((CHUNKS,)), dma((CHUNKS,)),
            dma((CHUNKS,)), dma((CHUNKS,)), dma((2,)), dma((2,)), dma((14,)), dma((14,)),
        ],
        compiler_params=pltpu.CompilerParams(
            collective_id=0, has_side_effects=True, vmem_limit_bytes=VMEM_LIMIT
        ),
        name="gram_step",
    )(gradient)
    return updates


def solution(mesh):
    return jax.shard_map(
        on_device,
        mesh=mesh,
        in_specs=(P("dp", "tensor", None),),
        out_specs=P(None, "tensor", None),
        check_vma=False,
    )
```

time: 134 us -> 53 us (0.40)
  the two profiles are of different devices: /device:TPU:6 before, /device:TPU:1 now
where the time goes in v2:
time: 53 us; the launch traced here: 52.6 us
  Pallas kernels  51.6 us (97%)
  local copies, waits for them, and re-layouts  0.97 us (2%)
    pallas_call x1, Pallas kernels, on_device(): pl.pallas_call(kernel, out_shape=pltpu.VMEM((8, B, OUTPUTS), bf16), in_sp...  51.6 us

profile of v2, /device:TPU:1, one launch (start us, length us, event | category | flops | bytes accessed | tf_op | source)
XLA Modules:
  0.0 52.6 jit_solution(14561117815086300723)
XLA Ops:
  0.0 51.6 %gram_step.1 = bf16[8,128,512]{2,1,0:T(8,128)(2,1)S(1)} custom-call(f32[1,128,512]{2,1,0:T(8,128)} %x_hbm.1), custom_call_target="tpu_custom_call" | custom-call | tf_op jit(solution)/shard_map/gram_step/pallas_call | solution.py:262
  51.6 1.0 %copy.3 = bf16[8,128,512]{2,1,0:T(8,128)(2,1)} copy(bf16[8,128,512]{2,1,0:T(8,128)(2,1)S(1)} %gram_step.1) | data formatting | bytes 2097152

commit v3 on v2

v3 whole, which is shorter than its diff:
```python
import math

import jax
import jax.numpy as jnp
from jax import lax
from jax.experimental import pallas as pl
from jax.experimental.pallas import tpu as pltpu
from jax.sharding import PartitionSpec as P

FEATURES = 8192
OUTPUTS = 512

linear_term = 3.4445
cubic_term = -4.775
quintic_term = 2.0315
norm_floor = 1e-07
update_gain = 0.2

NX, NZ, NY = 4, 8, 2
NEAR = NX * NY * 2
FAR = NZ // 2
HI = 4
B = 128
TILE = 8
TILES = 8
CHUNKS = [(0, 1), (1, 2), (2, 4), (4, 6), (6, 7), (7, 8)]
PARTS = 8
ROWS = B // PARTS
UPDATE_COPIES = 3 * PARTS
VMEM_LIMIT = 65850000
MESH = pl.DeviceIdType.MESH

f32 = jnp.float32
bf16 = jnp.bfloat16

BLOCKS = [(0, 0), (0, 1), (0, 2), (0, 3), (1, 2), (1, 3), (2, 2), (2, 3)]
EARLY = 6


def halves(value):
    high = value.astype(bf16)
    low = (value - high.astype(f32)).astype(bf16)
    return high, low


def mm(a, b):
    return jnp.dot(a, b, preferred_element_type=f32)


def product(a, b):
    (ah, al), (bh, bl) = a, b
    return mm(ah, bh) + (mm(ah, bl) + mm(al, bh))


def kernel(x_hbm, o_ref, x_ref, pk, r1, s1, r2, s2, r3, gf, e_own, e_line, e_near, e_all,
           g_ref, gh, gl, sq, x_sem, ss, v1, v2, v3, v4, ve, v5, vm):
    e1, e2, e3 = e_all.at[0], e_all.at[1], e_all.at[2]
    dp = lax.axis_index("dp")
    t = lax.axis_index("tensor")
    yl = lax.rem(t, NY)
    z = lax.rem(lax.div(t, NY), NZ)
    zl = lax.rem(z, 2)
    zh = lax.div(z, 2)
    xx = lax.div(t, NY * NZ)
    hi = lax.div(dp, 2)
    core = lax.rem(dp, 2)

    load = pltpu.make_async_copy(x_hbm.at[0], x_ref, x_sem)
    load.start()

    def at(x_, w_):
        return {"tensor": (x_ * NZ + zh * 2 + lax.rem(w_, 2)) * NY + lax.div(w_, 2)}

    w = yl * 2 + zl

    def square_peer(k):
        pw = lax.rem(yl + k // 2, NY) * 2 + lax.rem(zl + k % 2, 2)
        return pw, at(xx, pw)

    def line_peer(k):
        px = lax.rem(xx + k, NX)
        return px, at(px, w)

    def near_peer(k):
        px = lax.rem(xx + k // 4, NX)
        pw = lax.rem(yl + (k // 2) % 2, NY) * 2 + lax.rem(zl + k % 2, 2)
        return at(px, pw)

    def far_peer(k):
        return {"tensor": (xx * NZ + lax.rem(zh + k, FAR) * 2 + zl) * NY + yl}

    line = [line_peer(k) for k in range(1, NX)]
    square = [square_peer(k) for k in range(1, 4)]
    near = [near_peer(k) for k in range(1, NEAR)]
    far = [far_peer(k) for k in range(1, FAR)]
    d_right = lax.rem(hi + 1, HI) * 2 + core
    d_left = lax.rem(hi + HI - 1, HI) * 2 + core
    d_far = lax.rem(hi + 2, HI) * 2 + core
    mate = {"dp": hi * 2 + 1 - core}
    right = {"dp": d_right}
    left = {"dp": d_left}

    barrier = pltpu.get_barrier_semaphore()
    peers = far + [p for _, p in line] + [p for _, p in square] + [right, left, mate]
    for peer in peers:
        pl.semaphore_signal(barrier, inc=1, device_id=peer, device_id_type=MESH)
    with jax.named_scope("load"):
        load.wait()

    with jax.named_scope("gram_local"):
        x = x_ref[...]
        xh, xl = halves(x)
        xth, xtl = halves(x.T)
        row = lax.broadcasted_iota(jnp.int32, (B, B), 0)
        col = lax.broadcasted_iota(jnp.int32, (B, B), 1)
        rows = []
        for i in range(4):
            a, b = i * B, (i + 1) * B
            rows.append(
                mm(xth[a:b], xh[:, a:]) + (mm(xth[a:b], xl[:, a:]) + mm(xtl[a:b], xh[:, a:]))
            )

        def block(i, j):
            return rows[i][:, (j - i) * B:(j - i + 1) * B]

        for n, (i, j) in enumerate(BLOCKS):
            value = block(i, j)
            if i == j:
                value = jnp.where(col >= row, value, block(i + 1, i + 1))
            pk[n] = value.reshape(NX, 4, TILE, B)
        d1 = jnp.sum(jnp.where(row == col, block(1, 1), 0.0), axis=0, keepdims=True)
        d3 = jnp.sum(jnp.where(row == col, block(3, 3), 0.0), axis=0, keepdims=True)
        e_own[...] = jnp.concatenate([d1, d3], axis=0)

    with jax.named_scope("enter"):
        pl.semaphore_wait(barrier, len(peers))

    def remote(src, dst, send, recv, peer):
        copy = pltpu.make_async_remote_copy(
            src_ref=src, dst_ref=dst, send_sem=send, recv_sem=recv,
            device_id=peer, device_id_type=MESH,
        )
        copy.start()
        return copy

    def arrived(ref, sem):
        pltpu.make_async_remote_copy(
            src_ref=ref, dst_ref=ref, send_sem=sem, recv_sem=sem,
            device_id=mate, device_id_type=MESH,
        ).wait_recv()

    for k in range(3):
        remote(e_own, e1.at[k], ss.at[0], ve.at[0], line[k][1])
    for c, (a, b) in enumerate(CHUNKS):
        for n in range(a, b):
            for k in range(3):
                if n % 2 == 0:
                    place, peer = line[k]
                    piece = pk.at[n, place]
                else:
                    place, peer = square[k]
                    piece = pk.at[n, :, place]
                remote(piece, r1.at[n, k], ss.at[1], v1.at[c], peer)
    arrived(e1, ve.at[0])
    extra = e_own[...] + e1[0] + e1[1] + e1[2]
    e_line[...] = extra
    for k in range(3):
        remote(e_line, e2.at[k], ss.at[0], ve.at[1], square[k][1])
    for c, (a, b) in enumerate(CHUNKS):
        with jax.named_scope("one_%d" % c):
            arrived(r1.at[a:b], v1.at[c])
        for n in range(a, b):
            own = pk[n, xx] if n % 2 == 0 else pk[n, :, w]
            s1[n] = own + r1[n, 0] + r1[n, 1] + r1[n, 2]
            for k in range(3):
                place, peer = square[k] if n % 2 == 0 else line[k]
                remote(s1.at[n, place], r2.at[n, k], ss.at[2], v2.at[c], peer)
    arrived(e2, ve.at[1])
    extra = e_line[...] + e2[0] + e2[1] + e2[2]
    e_near[...] = extra
    for k in range(3):
        remote(e_near, e3.at[k], ss.at[0], ve.at[2], far[k])
    for c, (a, b) in enumerate(CHUNKS):
        with jax.named_scope("two_%d" % c):
            arrived(r2.at[a:b], v2.at[c])
        for n in range(a, b):
            own = s1[n, w] if n % 2 == 0 else s1[n, xx]
            s2[n] = own + r2[n, 0] + r2[n, 1] + r2[n, 2]
        for k in range(3):
            remote(s2.at[a:b], r3.at[k, a:b], ss.at[3], v3.at[c], far[k])
    for c, (a, b) in enumerate(CHUNKS):
        with jax.named_scope("far_%d" % c):
            arrived(r3.at[:, a:b], v3.at[c])
        gf[a:b, xx * 4 + w] = s2[a:b] + r3[0, a:b] + r3[1, a:b] + r3[2, a:b]
        for k in range(NEAR - 1):
            where = gf.at[a:b, xx * 4 + w]
            remote(where, where, ss.at[4], v4.at[c], near[k])
    arrived(e3, ve.at[2])
    extra = e_near[...] + e3[0] + e3[1] + e3[2]

    def put_block(i, j, value):
        rows, cols = slice(i * B, (i + 1) * B), slice(j * B, (j + 1) * B)
        g_ref[rows, cols] = value
        high, low = halves(value)
        gh[rows, cols] = high
        gl[rows, cols] = low

    trace = jnp.sum(extra, keepdims=True)
    half = OUTPUTS // 2

    def partial_square(a, b):
        return product((gh[:, a:b], gl[:, a:b]), (gh[a:b, :], gl[a:b, :]))

    for c, (a, b) in enumerate(CHUNKS):
        with jax.named_scope("gather_%d" % c):
            arrived(gf.at[a:b, 0:NEAR - 1], v4.at[c])
        for n in range(a, b):
            i, j = BLOCKS[n]
            here = gf[n].reshape(B, B)
            flip = here.T
            if i == j:
                trace = trace + jnp.sum(jnp.where(row == col, here, 0.0), keepdims=True)
                put_block(i, i, jnp.where(col >= row, here, flip))
                corner = jnp.broadcast_to(extra[i // 2:i // 2 + 1], (B, B))
                put_block(
                    i + 1, i + 1, jnp.where(row == col, corner, jnp.where(col < row, here, flip))
                )
            else:
                put_block(i, j, here)
                put_block(j, i, flip)
        if b == EARLY:
            sq[...] = partial_square(0, half)
    divisor = jnp.sqrt(trace) + norm_floor
    inverse = 1.0 / (divisor * divisor)
    factor = (update_gain * math.sqrt(max(FEATURES, OUTPUTS))) / divisor

    with jax.named_scope("chain"):
        identity = jnp.where(
            lax.broadcasted_iota(jnp.int32, (OUTPUTS, OUTPUTS), 0)
            == lax.broadcasted_iota(jnp.int32, (OUTPUTS, OUTPUTS), 1),
            linear_term,
            0.0,
        )
        tall = (xh, xl)
        gram = g_ref[...] * inverse
        poly = halves(
            identity + cubic_term * gram
            + (quintic_term * inverse * inverse) * (sq[...] + partial_square(half, OUTPUTS))
        )
        tall = halves(product(tall, poly))
        gram = inverse * product((gh[...], gl[...]), halves(product(poly, poly)))
        pair = halves(gram)
        poly = halves(identity + cubic_term * gram + quintic_term * product(pair, pair))
        tall = halves(product(tall, poly))
        gram = product(pair, halves(product(poly, poly)))
        pair = halves(gram)
        base = tall[0].astype(f32) + tall[1].astype(f32)
        once = product(tall, pair)
        twice = product(halves(once), pair)
        polished = linear_term * base + cubic_term * once + quintic_term * twice
        o_ref[dp] = (factor * polished).astype(bf16)

    count = iter(range(UPDATE_COPIES))

    def send(matrix, first, last, peer):
        where = o_ref.at[matrix, first * ROWS:last * ROWS]
        return remote(where, where, ss.at[5], v5.at[next(count)], peer)

    def send_mate(matrix, first, last):
        where = o_ref.at[matrix, first * ROWS:last * ROWS]
        remote(where, where, ss.at[5], vm.at[0], mate)

    half = PARTS // 2
    to_r, to_l = {}, {}
    for i in range(PARTS):
        j = (i + half) % PARTS
        to_r[i] = send(dp, i, i + 1, right)
        to_l[j] = send(dp, j, j + 1, left)
    send_mate(dp, 0, PARTS)
    on_r, on_l = {}, {}
    for i in range(half):
        j = i + half
        with jax.named_scope("u_near_%d" % i):
            to_r[i].wait_recv()
            on_r[i] = send(d_left, i, i + 1, right)
            to_l[j].wait_recv()
            on_l[j] = send(d_right, j, j + 1, left)
    send_mate(d_left, 0, half)
    send_mate(d_right, half, PARTS)
    for i in range(half):
        j = i + half
        with jax.named_scope("u_rest_%d" % i):
            to_r[j].wait_recv()
            to_l[i].wait_recv()
        if i == half - 1:
            send_mate(d_left, half, PARTS)
            send_mate(d_right, 0, half)
        with jax.named_scope("u_far_%d" % i):
            on_r[i].wait_recv()
            send_mate(d_far, i, i + 1)
            on_l[j].wait_recv()
            send_mate(d_far, j, j + 1)
    def left_all(ref, sem):
        pltpu.make_async_remote_copy(
            src_ref=ref, dst_ref=ref, send_sem=sem, recv_sem=sem,
            device_id=mate, device_id_type=MESH,
        ).wait_send()

    with jax.named_scope("u_mate"):
        arrived(o_ref.at[0:HI], vm.at[0])
    with jax.named_scope("drain"):
        left_all(e_all, ss.at[0])
        left_all(r1, ss.at[1])
        left_all(r2, ss.at[2])
        left_all(r3, ss.at[3])
        left_all(gf.at[:, 0:NEAR - 1], ss.at[4])
        left_all(o_ref.at[0:7], ss.at[5])


def on_device(gradient):
    dma = pltpu.SemaphoreType.DMA
    updates = pl.pallas_call(
        kernel,
        out_shape=pltpu.VMEM((8, B, OUTPUTS), bf16),
        in_specs=[pl.BlockSpec(memory_space=pltpu.HBM)],
        out_specs=pl.BlockSpec(memory_space=pltpu.VMEM),
        scratch_shapes=[
            pltpu.VMEM((B, OUTPUTS), f32),
            pltpu.VMEM((TILES, NX, 4, TILE, B), f32),
            pltpu.VMEM((TILES, 3, 4, TILE, B), f32),
            pltpu.VMEM((TILES, 4, TILE, B), f32),
            pltpu.VMEM((TILES, 3, TILE, B), f32),
            pltpu.VMEM((TILES, TILE, B), f32),
            pltpu.VMEM((3, TILES, TILE, B), f32),
            pltpu.VMEM((TILES, NEAR, TILE, B), f32),
            pltpu.VMEM((2, B), f32),
            pltpu.VMEM((2, B), f32),
            pltpu.VMEM((2, B), f32),
            pltpu.VMEM((3, 3, 2, B), f32),
            pltpu.VMEM((OUTPUTS, OUTPUTS), f32),
            pltpu.VMEM((OUTPUTS, OUTPUTS), bf16),
            pltpu.VMEM((OUTPUTS, OUTPUTS), bf16),
            pltpu.VMEM((OUTPUTS, OUTPUTS), f32),
            dma,
            dma((6,)),
            *[dma((len(CHUNKS),)) for _ in range(4)],
            dma((3,)), dma((UPDATE_COPIES,)), dma((1,)),
        ],
        compiler_params=pltpu.CompilerParams(
            collective_id=0, has_side_effects=True, vmem_limit_bytes=VMEM_LIMIT
        ),
        name="gram_step",
    )(gradient)
    return updates


def solution(mesh):
    return jax.shard_map(
        on_device,
        mesh=mesh,
        in_specs=(P("dp", "tensor", None),),
        out_specs=P(None, "tensor", None),
        check_vma=False,
    )
```

time: 53 us -> 51.8 us (0.977)
  Pallas kernels: 51.6 us -> 50.7 us
    pallas_call x1, Pallas kernels: 51.6 us -> 50.7 us  [on_device(): pl.pallas_call(kernel, out_shape=pltpu.VMEM((8, B, OUTPUTS), bf16), in_sp...]
where the time goes in v3:
time: 51.8 us; the launch traced here: 51.7 us
  Pallas kernels  50.7 us (98%)
  local copies, waits for them, and re-layouts  0.97 us (2%)
    pallas_call x1, Pallas kernels, on_device(): pl.pallas_call(kernel, out_shape=pltpu.VMEM((8, B, OUTPUTS), bf16), in_sp...  50.7 us

profile of v3, /device:TPU:1, one launch (start us, length us, event | category | flops | bytes accessed | tf_op | source)
XLA Modules:
  0.0 51.7 jit_solution(11777734837120795895)
XLA Ops:
  0.0 50.7 %gram_step.1 = bf16[8,128,512]{2,1,0:T(8,128)(2,1)S(1)} custom-call(f32[1,128,512]{2,1,0:T(8,128)} %x_hbm.1), custom_call_target="tpu_custom_call" | custom-call | tf_op jit(solution)/shard_map/gram_step/pallas_call | solution.py:322
  50.7 1.0 %copy.3 = bf16[8,128,512]{2,1,0:T(8,128)(2,1)} copy(bf16[8,128,512]{2,1,0:T(8,128)(2,1)S(1)} %gram_step.1) | data formatting | bytes 2097152

commit v4 on v3

--- a/solution.py
+++ b/solution.py
@@ -24,9 +24,7 @@
 TILE = 8
 TILES = 8
 CHUNKS = [(0, 1), (1, 2), (2, 4), (4, 6), (6, 7), (7, 8)]
-PARTS = 8
-ROWS = B // PARTS
-UPDATE_COPIES = 3 * PARTS
+PARTS0, PARTS1 = 8, 4
 VMEM_LIMIT = 65850000
 MESH = pl.DeviceIdType.MESH
 
@@ -53,7 +51,7 @@
 
 
 def kernel(x_hbm, o_ref, x_ref, pk, r1, s1, r2, s2, r3, gf, e_own, e_line, e_near, e_all,
-           g_ref, gh, gl, sq, x_sem, ss, v1, v2, v3, v4, ve, v5, vm):
+           g_ref, gh, gl, sq, ph, pl_, qh, ql, nh, nl, gh2, gl2, x_sem, ss, v1, v2, v3, v4, ve, vu0, vu1, vm):
     e1, e2, e3 = e_all.at[0], e_all.at[1], e_all.at[2]
     dp = lax.axis_index("dp")
     t = lax.axis_index("tensor")
@@ -93,17 +91,25 @@
     square = [square_peer(k) for k in range(1, 4)]
     near = [near_peer(k) for k in range(1, NEAR)]
     far = [far_peer(k) for k in range(1, FAR)]
-    d_right = lax.rem(hi + 1, HI) * 2 + core
-    d_left = lax.rem(hi + HI - 1, HI) * 2 + core
-    d_far = lax.rem(hi + 2, HI) * 2 + core
+    h_right, h_left, h_far = (lax.rem(hi + k, HI) for k in (1, HI - 1, 2))
     mate = {"dp": hi * 2 + 1 - core}
-    right = {"dp": d_right}
-    left = {"dp": d_left}
+    right = {"dp": h_right * 2 + 1}
+    left = {"dp": h_left * 2 + 1}
 
     barrier = pltpu.get_barrier_semaphore()
-    peers = far + [p for _, p in line] + [p for _, p in square] + [right, left, mate]
-    for peer in peers:
+
+    def greet(peer):
         pl.semaphore_signal(barrier, inc=1, device_id=peer, device_id_type=MESH)
+
+    for peer in far + [p for _, p in line] + [p for _, p in square] + [mate]:
+        greet(peer)
+
+    @pl.when(core == 1)
+    def _():
+        for h in (h_right, h_left):
+            for c in range(2):
+                greet({"dp": h * 2 + c})
+
     with jax.named_scope("load"):
         load.wait()
 
@@ -133,7 +139,7 @@
         e_own[...] = jnp.concatenate([d1, d3], axis=0)
 
     with jax.named_scope("enter"):
-        pl.semaphore_wait(barrier, len(peers))
+        pl.semaphore_wait(barrier, 12)
 
     def remote(src, dst, send, recv, peer):
         copy = pltpu.make_async_remote_copy(
@@ -208,9 +214,6 @@
     trace = jnp.sum(extra, keepdims=True)
     half = OUTPUTS // 2
 
-    def partial_square(a, b):
-        return product((gh[:, a:b], gl[:, a:b]), (gh[a:b, :], gl[a:b, :]))
-
     for c, (a, b) in enumerate(CHUNKS):
         with jax.named_scope("gather_%d" % c):
             arrived(gf.at[a:b, 0:NEAR - 1], v4.at[c])
@@ -229,92 +232,162 @@
                 put_block(i, j, here)
                 put_block(j, i, flip)
         if b == EARLY:
-            sq[...] = partial_square(0, half)
+            for i, j in ((slice(0, half), slice(0, OUTPUTS)), (slice(half, OUTPUTS), slice(half, OUTPUTS))):
+                sq[i, j] = product((gh[i, :half], gl[i, :half]), (gh[:half, j], gl[:half, j]))
     divisor = jnp.sqrt(trace) + norm_floor
     inverse = 1.0 / (divisor * divisor)
     factor = (update_gain * math.sqrt(max(FEATURES, OUTPUTS))) / divisor
 
     with jax.named_scope("chain"):
-        identity = jnp.where(
-            lax.broadcasted_iota(jnp.int32, (OUTPUTS, OUTPUTS), 0)
-            == lax.broadcasted_iota(jnp.int32, (OUTPUTS, OUTPUTS), 1),
+        near_half, far_half = slice(0, half), slice(half, OUTPUTS)
+        spots = ((near_half, far_half), (far_half, far_half), (near_half, near_half))
+        eye = jnp.where(
+            lax.broadcasted_iota(jnp.int32, (half, half), 0)
+            == lax.broadcasted_iota(jnp.int32, (half, half), 1),
             linear_term,
             0.0,
         )
+
+        def times(p, r, i, j):
+            return sum(
+                product((p[0][i, k], p[1][i, k]), (r[0][k, j], r[1][k, j]))
+                for k in (far_half, near_half)
+            )
+
+        def keep(pair, i, j, value):
+            high, low = halves(value)
+            pair[0][i, j], pair[1][i, j] = high, low
+            if i != j:
+                pair[0][j, i], pair[1][j, i] = high.T, low.T
+
+        def whole(pair):
+            return pair[0][...], pair[1][...]
+
+        gram, poly, poly2 = (gh, gl), (ph, pl_), (qh, ql)
         tall = (xh, xl)
-        gram = g_ref[...] * inverse
-        poly = halves(
-            identity + cubic_term * gram
-            + (quintic_term * inverse * inverse) * (sq[...] + partial_square(half, OUTPUTS))
-        )
-        tall = halves(product(tall, poly))
-        gram = inverse * product((gh[...], gl[...]), halves(product(poly, poly)))
-        pair = halves(gram)
-        poly = halves(identity + cubic_term * gram + quintic_term * product(pair, pair))
-        tall = halves(product(tall, poly))
-        gram = product(pair, halves(product(poly, poly)))
-        pair = halves(gram)
+        for turn in range(2):
+            for i, j in spots:
+                if turn == 0:
+                    square = sq[i, j] + product(
+                        (gh[i, half:], gl[i, half:]), (gh[half:, j], gl[half:, j])
+                    )
+                    value = (cubic_term * inverse) * g_ref[i, j] + (
+                        quintic_term * inverse * inverse
+                    ) * square
+                else:
+                    value = cubic_term * g_ref[i, j] + quintic_term * times(gram, gram, i, j)
+                keep(poly, i, j, eye + value if i == j else value)
+            for i, j in spots:
+                keep(poly2, i, j, times(poly, poly, i, j))
+            tall = halves(product(tall, whole(poly)))
+            for i, j in spots:
+                value = times(gram, poly2, i, j)
+                if turn == 0:
+                    value = inverse * value
+                fresh = (nh, nl) if turn == 0 else (gh2, gl2)
+                keep(fresh, i, j, value)
+                g_ref[i, j] = value
+            gram = fresh
         base = tall[0].astype(f32) + tall[1].astype(f32)
-        once = product(tall, pair)
-        twice = product(halves(once), pair)
+
+        def thin(pair, j, order):
+            return sum(
+                product((pair[0][:, k], pair[1][:, k]), (gram[0][k, j], gram[1][k, j]))
+                for k in order
+            )
+
+        once = [thin(tall, j, (far_half, near_half)) for j in (near_half, far_half)]
+        pair = [jnp.concatenate(p, axis=1) for p in zip(*(halves(o) for o in once))]
+        twice = [thin(pair, j, (near_half, far_half)) for j in (near_half, far_half)]
+        once, twice = jnp.concatenate(once, axis=1), jnp.concatenate(twice, axis=1)
         polished = linear_term * base + cubic_term * once + quintic_term * twice
         o_ref[dp] = (factor * polished).astype(bf16)
 
-    count = iter(range(UPDATE_COPIES))
-
-    def send(matrix, first, last, peer):
-        where = o_ref.at[matrix, first * ROWS:last * ROWS]
-        return remote(where, where, ss.at[5], v5.at[next(count)], peer)
+    def part(matrix, first, last):
+        return o_ref.at[matrix, first:last]
+
+    def send(matrix, first, last, sem, peer):
+        where = part(matrix, first, last)
+        remote(where, where, ss.at[5], sem, peer)
 
     def send_mate(matrix, first, last):
-        where = o_ref.at[matrix, first * ROWS:last * ROWS]
-        remote(where, where, ss.at[5], vm.at[0], mate)
-
-    half = PARTS // 2
-    to_r, to_l = {}, {}
-    for i in range(PARTS):
-        j = (i + half) % PARTS
-        to_r[i] = send(dp, i, i + 1, right)
-        to_l[j] = send(dp, j, j + 1, left)
-    send_mate(dp, 0, PARTS)
-    on_r, on_l = {}, {}
-    for i in range(half):
-        j = i + half
-        with jax.named_scope("u_near_%d" % i):
-            to_r[i].wait_recv()
-            on_r[i] = send(d_left, i, i + 1, right)
-            to_l[j].wait_recv()
-            on_l[j] = send(d_right, j, j + 1, left)
-    send_mate(d_left, 0, half)
-    send_mate(d_right, half, PARTS)
-    for i in range(half):
-        j = i + half
-        with jax.named_scope("u_rest_%d" % i):
-            to_r[j].wait_recv()
-            to_l[i].wait_recv()
-        if i == half - 1:
-            send_mate(d_left, half, PARTS)
-            send_mate(d_right, 0, half)
-        with jax.named_scope("u_far_%d" % i):
-            on_r[i].wait_recv()
-            send_mate(d_far, i, i + 1)
-            on_l[j].wait_recv()
-            send_mate(d_far, j, j + 1)
+        where = part(matrix, first, last)
+        remote(where, where, ss.at[6], vm.at[0], mate)
+
     def left_all(ref, sem):
         pltpu.make_async_remote_copy(
             src_ref=ref, dst_ref=ref, send_sem=sem, recv_sem=sem,
             device_id=mate, device_id_type=MESH,
         ).wait_send()
 
-    with jax.named_scope("u_mate"):
-        arrived(o_ref.at[0:HI], vm.at[0])
+    def rows_of(i, parts):
+        j = (i + parts // 2) % parts
+        n = B // parts
+        return (i * n, (i + 1) * n), (j * n, (j + 1) * n)
+
+    def send_own(parts, sems):
+        for i in range(parts):
+            first, second = rows_of(i, parts)
+            send(dp, *first, sems.at[i], right)
+            send(dp, *second, sems.at[i], left)
+        send_mate(dp, 0, B)
+
+    def from_near(i, parts, sems, c, onward):
+        first, second = rows_of(i, parts)
+        m_left, m_right = h_left * 2 + c, h_right * 2 + c
+        arrived(part(0, 0, 2 * B // parts), sems.at[i])
+        if onward:
+            send(m_left, *first, sems.at[parts + i], right)
+            send(m_right, *second, sems.at[parts + i], left)
+        send_mate(m_left, *first)
+        send_mate(m_right, *second)
+
+    def from_far(i, parts, sems, c):
+        first, second = rows_of(i, parts)
+        arrived(part(0, 0, 2 * B // parts), sems.at[parts + i])
+        send_mate(h_far * 2 + c, *first)
+        send_mate(h_far * 2 + c, *second)
+
+    @pl.when(core == 0)
+    def _():
+        send_own(PARTS0, vu0)
+        with jax.named_scope("u_mate0"):
+            arrived(o_ref.at[0:7], vm.at[0])
+        left_all(o_ref.at[0:2], ss.at[5])
+        left_all(o_ref.at[0:1], ss.at[6])
+
+    @pl.when(core == 1)
+    def _():
+        send_own(PARTS1, vu1)
+        with jax.named_scope("n_near1"):
+            for i in range(PARTS1 // 2):
+                from_near(i, PARTS1, vu1, 1, True)
+        with jax.named_scope("n_rest1"):
+            for i in range(PARTS1 // 2, PARTS1):
+                from_near(i, PARTS1, vu1, 1, False)
+        with jax.named_scope("n_near0"):
+            for i in range(PARTS0 // 2):
+                from_near(i, PARTS0, vu0, 0, True)
+        with jax.named_scope("n_far1"):
+            for i in range(PARTS1 // 2):
+                from_far(i, PARTS1, vu1, 1)
+        with jax.named_scope("n_rest0"):
+            for i in range(PARTS0 // 2, PARTS0):
+                from_near(i, PARTS0, vu0, 0, False)
+        with jax.named_scope("n_far0"):
+            for i in range(PARTS0 // 2):
+                from_far(i, PARTS0, vu0, 0)
+        with jax.named_scope("n_mate"):
+            arrived(o_ref.at[0:1], vm.at[0])
+            left_all(o_ref.at[0:4], ss.at[5])
+            left_all(o_ref.at[0:7], ss.at[6])
+
     with jax.named_scope("drain"):
         left_all(e_all, ss.at[0])
         left_all(r1, ss.at[1])
         left_all(r2, ss.at[2])
         left_all(r3, ss.at[3])
         left_all(gf.at[:, 0:NEAR - 1], ss.at[4])
-        left_all(o_ref.at[0:7], ss.at[5])
 
 
 def on_device(gradient):
@@ -341,10 +414,11 @@
             pltpu.VMEM((OUTPUTS, OUTPUTS), bf16),
             pltpu.VMEM((OUTPUTS, OUTPUTS), bf16),
             pltpu.VMEM((OUTPUTS, OUTPUTS), f32),
+            *[pltpu.VMEM((OUTPUTS, OUTPUTS), bf16) for _ in range(8)],
             dma,
-            dma((6,)),
+            dma((7,)),
             *[dma((len(CHUNKS),)) for _ in range(4)],
-            dma((3,)), dma((UPDATE_COPIES,)), dma((1,)),
+            dma((3,)), dma((PARTS0 * 3 // 2,)), dma((PARTS1 * 3 // 2,)), dma((1,)),
         ],
         compiler_params=pltpu.CompilerParams(
             collective_id=0, has_side_effects=True, vmem_limit_bytes=VMEM_LIMIT

time: 51.8 us -> 50.3 us (0.971)
  Pallas kernels: 50.7 us -> 49.2 us
    pallas_call x1, Pallas kernels: 50.7 us -> 49.2 us  [on_device(): pl.pallas_call(kernel, out_shape=pltpu.VMEM((8, B, OUTPUTS), bf16), in_sp...]
where the time goes in v4:
time: 50.3 us; the launch traced here: 50.2 us
  Pallas kernels  49.2 us (98%)
  local copies, waits for them, and re-layouts  0.97 us (2%)
    pallas_call x1, Pallas kernels, on_device(): pl.pallas_call(kernel, out_shape=pltpu.VMEM((8, B, OUTPUTS), bf16), in_sp...  49.2 us

profile of v4, /device:TPU:1, one launch (start us, length us, event | category | flops | bytes accessed | tf_op | source)
XLA Modules:
  0.0 50.2 jit_solution(14722572053123481148)
XLA Ops:
  0.0 49.2 %gram_step.1 = bf16[8,128,512]{2,1,0:T(8,128)(2,1)S(1)} custom-call(f32[1,128,512]{2,1,0:T(8,128)} %x_hbm.1), custom_call_target="tpu_custom_call" | custom-call | tf_op jit(solution)/shard_map/gram_step/pallas_call | solution.py:395
  49.2 1.0 %copy.3 = bf16[8,128,512]{2,1,0:T(8,128)(2,1)} copy(bf16[8,128,512]{2,1,0:T(8,128)(2,1)S(1)} %gram_step.1) | data formatting | bytes 2097152

commit v5 on v4

--- a/solution.py
+++ b/solution.py
@@ -23,7 +23,7 @@
 B = 128
 TILE = 8
 TILES = 8
-CHUNKS = [(0, 1), (1, 2), (2, 4), (4, 6), (6, 7), (7, 8)]
+CHUNKS = [(0, 2), (2, 4), (4, 6), (6, 8)]
 PARTS0, PARTS1 = 8, 4
 VMEM_LIMIT = 65850000
 MESH = pl.DeviceIdType.MESH
@@ -50,8 +50,8 @@
     return mm(ah, bh) + (mm(ah, bl) + mm(al, bh))
 
 
-def kernel(x_hbm, o_ref, x_ref, pk, r1, s1, r2, s2, r3, gf, e_own, e_line, e_near, e_all,
-           g_ref, gh, gl, sq, ph, pl_, qh, ql, nh, nl, gh2, gl2, x_sem, ss, v1, v2, v3, v4, ve, vu0, vu1, vm):
+def kernel(x_hbm, o_ref, x_ref, pk, r1, s1, r2, s2, s3, r3, gf, e_own, e_line, e_near, e_two, e_sum, e_all,
+           g_ref, gh, gl, sq, ph, pl_, qh, ql, nh, nl, gh2, gl2, x_sem, ss, v1, v2, v3, v4, v5, ve, vu0, vu1, vm):
     e1, e2, e3 = e_all.at[0], e_all.at[1], e_all.at[2]
     dp = lax.axis_index("dp")
     t = lax.axis_index("tensor")
@@ -84,13 +84,17 @@
         pw = lax.rem(yl + (k // 2) % 2, NY) * 2 + lax.rem(zl + k % 2, 2)
         return at(px, pw)
 
-    def far_peer(k):
-        return {"tensor": (xx * NZ + lax.rem(zh + k, FAR) * 2 + zl) * NY + yl}
+    def pair_peer(pair):
+        return {"tensor": (xx * NZ + pair * 2 + zl) * NY + yl}
+
+    late = lax.div(zh, 2)
+    partner = pair_peer(zh + 1 - 2 * lax.rem(zh, 2))
+    across = pair_peer(FAR - 1 - zh)
+    opposite = pair_peer(lax.rem(zh + 2, FAR))
 
     line = [line_peer(k) for k in range(1, NX)]
     square = [square_peer(k) for k in range(1, 4)]
     near = [near_peer(k) for k in range(1, NEAR)]
-    far = [far_peer(k) for k in range(1, FAR)]
     h_right, h_left, h_far = (lax.rem(hi + k, HI) for k in (1, HI - 1, 2))
     mate = {"dp": hi * 2 + 1 - core}
     right = {"dp": h_right * 2 + 1}
@@ -101,8 +105,12 @@
     def greet(peer):
         pl.semaphore_signal(barrier, inc=1, device_id=peer, device_id_type=MESH)
 
-    for peer in far + [p for _, p in line] + [p for _, p in square] + [mate]:
+    for peer in [across, partner] + [p for _, p in line] + [p for _, p in square] + [mate]:
         greet(peer)
+
+    @pl.when(late == 0)
+    def _():
+        greet(opposite)
 
     @pl.when(core == 1)
     def _():
@@ -139,7 +147,7 @@
         e_own[...] = jnp.concatenate([d1, d3], axis=0)
 
     with jax.named_scope("enter"):
-        pl.semaphore_wait(barrier, 12)
+        pl.semaphore_wait(barrier, 11 + late)
 
     def remote(src, dst, send, recv, peer):
         copy = pltpu.make_async_remote_copy(
@@ -184,25 +192,68 @@
     arrived(e2, ve.at[1])
     extra = e_line[...] + e2[0] + e2[1] + e2[2]
     e_near[...] = extra
-    for k in range(3):
-        remote(e_near, e3.at[k], ss.at[0], ve.at[2], far[k])
+    remote(e_near, e3.at[0], ss.at[7], ve.at[2], partner)
+
+    @pl.when(late == 1)
+    def _():
+        remote(e_near, e3.at[1], ss.at[7], ve.at[3], across)
+        remote(e_near, e3.at[2], ss.at[7], ve.at[3], opposite)
+
     for c, (a, b) in enumerate(CHUNKS):
         with jax.named_scope("two_%d" % c):
             arrived(r2.at[a:b], v2.at[c])
         for n in range(a, b):
             own = s1[n, w] if n % 2 == 0 else s1[n, xx]
             s2[n] = own + r2[n, 0] + r2[n, 1] + r2[n, 2]
-        for k in range(3):
-            remote(s2.at[a:b], r3.at[k, a:b], ss.at[3], v3.at[c], far[k])
+        mine = s2.at[a:b]
+        remote(mine, r3.at[0, a:b], ss.at[3], v3.at[c], partner)
+
+        @pl.when(late == 1)
+        def _():
+            remote(mine, r3.at[1, a:b], ss.at[3], v5.at[c], across)
+            remote(mine, r3.at[2, a:b], ss.at[3], v5.at[c], opposite)
+
+    @pl.when(late == 0)
+    def _():
+        arrived(e3.at[0], ve.at[2])
+        e_two[...] = e_near[...] + e3[0]
+        remote(e_two, e3.at[1], ss.at[7], ve.at[3], across)
+        for c, (a, b) in enumerate(CHUNKS):
+            arrived(r3.at[0, a:b], v3.at[c])
+            s3[a:b] = s2[a:b] + r3[0, a:b]
+            remote(s3.at[a:b], r3.at[1, a:b], ss.at[3], v5.at[c], across)
+
+    me = xx * 4 + w
     for c, (a, b) in enumerate(CHUNKS):
         with jax.named_scope("far_%d" % c):
-            arrived(r3.at[:, a:b], v3.at[c])
-        gf[a:b, xx * 4 + w] = s2[a:b] + r3[0, a:b] + r3[1, a:b] + r3[2, a:b]
+
+            @pl.when(late == 0)
+            def _():
+                arrived(r3.at[1:3, a:b], v5.at[c])
+                gf[a:b, me] = s3[a:b] + r3[1, a:b] + r3[2, a:b]
+
+            @pl.when(late == 1)
+            def _():
+                arrived(r3.at[0, a:b], v3.at[c])
+                arrived(r3.at[1, a:b], v5.at[c])
+                gf[a:b, me] = s2[a:b] + r3[0, a:b] + r3[1, a:b]
+
         for k in range(NEAR - 1):
-            where = gf.at[a:b, xx * 4 + w]
+            where = gf.at[a:b, me]
             remote(where, where, ss.at[4], v4.at[c], near[k])
-    arrived(e3, ve.at[2])
-    extra = e_near[...] + e3[0] + e3[1] + e3[2]
+
+    @pl.when(late == 0)
+    def _():
+        arrived(e3.at[1:3], ve.at[3])
+        e_sum[...] = e_two[...] + e3[1] + e3[2]
+
+    @pl.when(late == 1)
+    def _():
+        arrived(e3.at[0], ve.at[2])
+        arrived(e3.at[1], ve.at[3])
+        e_sum[...] = e_near[...] + e3[0] + e3[1]
+
+    extra = e_sum[...]
 
     def put_block(i, j, value):
         rows, cols = slice(i * B, (i + 1) * B), slice(j * B, (j + 1) * B)
@@ -383,10 +434,20 @@
             left_all(o_ref.at[0:7], ss.at[6])
 
     with jax.named_scope("drain"):
-        left_all(e_all, ss.at[0])
+        left_all(e_all.at[0:2], ss.at[0])
         left_all(r1, ss.at[1])
         left_all(r2, ss.at[2])
-        left_all(r3, ss.at[3])
+
+        @pl.when(late == 0)
+        def _():
+            left_all(r3.at[0:2], ss.at[3])
+            left_all(e3.at[0:2], ss.at[7])
+
+        @pl.when(late == 1)
+        def _():
+            left_all(r3, ss.at[3])
+            left_all(e3, ss.at[7])
+
         left_all(gf.at[:, 0:NEAR - 1], ss.at[4])
 
 
@@ -404,11 +465,10 @@
             pltpu.VMEM((TILES, 4, TILE, B), f32),
             pltpu.VMEM((TILES, 3, TILE, B), f32),
             pltpu.VMEM((TILES, TILE, B), f32),
+            pltpu.VMEM((TILES, TILE, B), f32),
             pltpu.VMEM((3, TILES, TILE, B), f32),
             pltpu.VMEM((TILES, NEAR, TILE, B), f32),
-            pltpu.VMEM((2, B), f32),
-            pltpu.VMEM((2, B), f32),
-            pltpu.VMEM((2, B), f32),
+            *[pltpu.VMEM((2, B), f32) for _ in range(5)],
             pltpu.VMEM((3, 3, 2, B), f32),
             pltpu.VMEM((OUTPUTS, OUTPUTS), f32),
             pltpu.VMEM((OUTPUTS, OUTPUTS), bf16),
@@ -416,9 +476,9 @@
             pltpu.VMEM((OUTPUTS, OUTPUTS), f32),
             *[pltpu.VMEM((OUTPUTS, OUTPUTS), bf16) for _ in range(8)],
             dma,
-            dma((7,)),
-            *[dma((len(CHUNKS),)) for _ in range(4)],
-            dma((3,)), dma((PARTS0 * 3 // 2,)), dma((PARTS1 * 3 // 2,)), dma((1,)),
+            dma((8,)),
+            *[dma((len(CHUNKS),)) for _ in range(5)],
+            dma((4,)), dma((PARTS0 * 3 // 2,)), dma((PARTS1 * 3 // 2,)), dma((1,)),
         ],
         compiler_params=pltpu.CompilerParams(
             collective_id=0, has_side_effects=True, vmem_limit_bytes=VMEM_LIMIT

time: 50.3 us -> 48.7 us (0.968)
  Pallas kernels: 49.2 us -> 47.5 us
    pallas_call x1, Pallas kernels: 49.2 us -> 47.5 us  [on_device(): pl.pallas_call(kernel, out_shape=pltpu.VMEM((8, B, OUTPUTS), bf16), in_sp...]
where the time goes in v5:
time: 48.7 us; the launch traced here: 48.5 us
  Pallas kernels  47.5 us (98%)
  local copies, waits for them, and re-layouts  0.97 us (2%)
    pallas_call x1, Pallas kernels, on_device(): pl.pallas_call(kernel, out_shape=pltpu.VMEM((8, B, OUTPUTS), bf16), in_sp...  47.5 us

profile of v5, /device:TPU:1, one launch (start us, length us, event | category | flops | bytes accessed | tf_op | source)
XLA Modules:
  0.0 48.5 jit_solution(4947878545136242158)
XLA Ops:
  0.0 47.5 %gram_step.1 = bf16[8,128,512]{2,1,0:T(8,128)(2,1)S(1)} custom-call(f32[1,128,512]{2,1,0:T(8,128)} %x_hbm.1), custom_call_target="tpu_custom_call" | custom-call | tf_op jit(solution)/shard_map/gram_step/pallas_call | solution.py:456
  47.6 1.0 %copy.3 = bf16[8,128,512]{2,1,0:T(8,128)(2,1)} copy(bf16[8,128,512]{2,1,0:T(8,128)(2,1)S(1)} %gram_step.1) | data formatting | bytes 2097152

commit v6 on v5

--- a/solution.py
+++ b/solution.py
@@ -51,7 +51,7 @@
 
 
 def kernel(x_hbm, o_ref, x_ref, pk, r1, s1, r2, s2, s3, r3, gf, e_own, e_line, e_near, e_two, e_sum, e_all,
-           g_ref, gh, gl, sq, ph, pl_, qh, ql, nh, nl, gh2, gl2, x_sem, ss, v1, v2, v3, v4, v5, ve, vu0, vu1, vm):
+           g_ref, gh, gl, sq, ph, pl_, qh, ql, rh, rl, nh, nl, gh2, gl2, x_sem, ss, v1, v2, v3, v4, v5, ve, vu0, vu1, vm):
     e1, e2, e3 = e_all.at[0], e_all.at[1], e_all.at[2]
     dp = lax.axis_index("dp")
     t = lax.axis_index("tensor")
@@ -315,42 +315,44 @@
             return pair[0][...], pair[1][...]
 
         gram, poly, poly2 = (gh, gl), (ph, pl_), (qh, ql)
-        tall = (xh, xl)
-        for turn in range(2):
-            for i, j in spots:
-                if turn == 0:
-                    square = sq[i, j] + product(
-                        (gh[i, half:], gl[i, half:]), (gh[half:, j], gl[half:, j])
-                    )
-                    value = (cubic_term * inverse) * g_ref[i, j] + (
-                        quintic_term * inverse * inverse
-                    ) * square
-                else:
-                    value = cubic_term * g_ref[i, j] + quintic_term * times(gram, gram, i, j)
-                keep(poly, i, j, eye + value if i == j else value)
-            for i, j in spots:
-                keep(poly2, i, j, times(poly, poly, i, j))
-            tall = halves(product(tall, whole(poly)))
-            for i, j in spots:
-                value = times(gram, poly2, i, j)
-                if turn == 0:
-                    value = inverse * value
-                fresh = (nh, nl) if turn == 0 else (gh2, gl2)
-                keep(fresh, i, j, value)
-                g_ref[i, j] = value
-            gram = fresh
-        base = tall[0].astype(f32) + tall[1].astype(f32)
-
-        def thin(pair, j, order):
-            return sum(
-                product((pair[0][:, k], pair[1][:, k]), (gram[0][k, j], gram[1][k, j]))
-                for k in order
-            )
-
-        once = [thin(tall, j, (far_half, near_half)) for j in (near_half, far_half)]
-        pair = [jnp.concatenate(p, axis=1) for p in zip(*(halves(o) for o in once))]
-        twice = [thin(pair, j, (near_half, far_half)) for j in (near_half, far_half)]
-        once, twice = jnp.concatenate(once, axis=1), jnp.concatenate(twice, axis=1)
+        both = (near_half, far_half)
+        rows0 = [(xh[:, k], xl[:, k]) for k in both]
+        rows1, rows2 = [None, None], [None, None]
+
+        def thin(rows, pair, n, order=(1, 0)):
+            j = both[n]
+            return sum(product(rows[k], (pair[0][both[k], j], pair[1][both[k], j])) for k in order)
+
+        for i, j in spots:
+            square = sq[i, j] + product((gh[i, half:], gl[i, half:]), (gh[half:, j], gl[half:, j]))
+            value = (cubic_term * inverse) * g_ref[i, j] + (
+                quintic_term * inverse * inverse
+            ) * square
+            keep(poly, i, j, eye + value if i == j else value)
+        for i, j in spots:
+            keep(poly2, i, j, times(poly, poly, i, j))
+        for i, j in spots:
+            value = inverse * times(gram, poly2, i, j)
+            keep((nh, nl), i, j, value)
+            g_ref[i, j] = value
+        gram = (nh, nl)
+        rows1[0] = halves(thin(rows0, poly, 0))
+        for i, j in spots:
+            value = cubic_term * g_ref[i, j] + quintic_term * times(gram, gram, i, j)
+            keep((rh, rl), i, j, eye + value if i == j else value)
+        rows1[1] = halves(thin(rows0, poly, 1))
+        for i, j in spots:
+            keep(poly2, i, j, times((rh, rl), (rh, rl), i, j))
+        rows2[0] = halves(thin(rows1, (rh, rl), 0))
+        for i, j in spots:
+            keep((gh2, gl2), i, j, times(gram, poly2, i, j))
+        gram = (gh2, gl2)
+        rows2[1] = halves(thin(rows1, (rh, rl), 1))
+        base = [h.astype(f32) + l.astype(f32) for h, l in rows2]
+        once = [thin(rows2, gram, n) for n in (0, 1)]
+        pairs = [halves(o) for o in once]
+        twice = [thin(pairs, gram, n, (0, 1)) for n in (0, 1)]
+        base, once, twice = (jnp.concatenate(v, axis=1) for v in (base, once, twice))
         polished = linear_term * base + cubic_term * once + quintic_term * twice
         o_ref[dp] = (factor * polished).astype(bf16)
 
@@ -474,7 +476,7 @@
             pltpu.VMEM((OUTPUTS, OUTPUTS), bf16),
             pltpu.VMEM((OUTPUTS, OUTPUTS), bf16),
             pltpu.VMEM((OUTPUTS, OUTPUTS), f32),
-            *[pltpu.VMEM((OUTPUTS, OUTPUTS), bf16) for _ in range(8)],
+            *[pltpu.VMEM((OUTPUTS, OUTPUTS), bf16) for _ in range(10)],
             dma,
             dma((8,)),
             *[dma((len(CHUNKS),)) for _ in range(5)],

time: 48.7 us -> 48.4 us (level)
  no operation moved by 1% of the time
where the time goes in v6:
time: 48.4 us; the launch traced here: 48.3 us
  Pallas kernels  47.3 us (98%)
  local copies, waits for them, and re-layouts  0.97 us (2%)
    pallas_call x1, Pallas kernels, on_device(): pl.pallas_call(kernel, out_shape=pltpu.VMEM((8, B, OUTPUTS), bf16), in_sp...  47.3 us
    unnamed x1, local copies, waits for them, and re-layouts  0.97 us

profile of v6, /device:TPU:1, one launch (start us, length us, event | category | flops | bytes accessed | tf_op | source)
XLA Modules:
  0.0 48.3 jit_solution(489850571182012360)
XLA Ops:
  0.0 47.3 %gram_step.1 = bf16[8,128,512]{2,1,0:T(8,128)(2,1)S(1)} custom-call(f32[1,128,512]{2,1,0:T(8,128)} %x_hbm.1), custom_call_target="tpu_custom_call" | custom-call | tf_op jit(solution)/shard_map/gram_step/pallas_call | solution.py:458
  47.3 1.0 %copy.3 = bf16[8,128,512]{2,1,0:T(8,128)(2,1)} copy(bf16[8,128,512]{2,1,0:T(8,128)(2,1)S(1)} %gram_step.1) | data formatting | bytes 2097152

commit v7 on v6

--- a/solution.py
+++ b/solution.py
@@ -51,7 +51,7 @@
 
 
 def kernel(x_hbm, o_ref, x_ref, pk, r1, s1, r2, s2, s3, r3, gf, e_own, e_line, e_near, e_two, e_sum, e_all,
-           g_ref, gh, gl, sq, ph, pl_, qh, ql, rh, rl, nh, nl, gh2, gl2, x_sem, ss, v1, v2, v3, v4, v5, ve, vu0, vu1, vm):
+           g_ref, gh, gl, sq, ph, pl_, qh, ql, rh, rl, nh, nl, gh2, gl2, sized, e_sized, x_sem, ss, v1, v2, v3, v4, v5, ve, vu0, vu1, vm):
     e1, e2, e3 = e_all.at[0], e_all.at[1], e_all.at[2]
     dp = lax.axis_index("dp")
     t = lax.axis_index("tensor")
@@ -94,7 +94,9 @@
 
     line = [line_peer(k) for k in range(1, NX)]
     square = [square_peer(k) for k in range(1, 4)]
-    near = [near_peer(k) for k in range(1, NEAR)]
+    hops = lambda k: (0, 1, 2, 1)[k // 4] + k // 2 % 2 + k % 2
+    near = [near_peer(k) for k in sorted(range(1, NEAR), key=hops, reverse=True)]
+    line_order, square_order = (1, 0, 2), (2, 0, 1)
     h_right, h_left, h_far = (lax.rem(hi + k, HI) for k in (1, HI - 1, 2))
     mate = {"dp": hi * 2 + 1 - core}
     right = {"dp": h_right * 2 + 1}
@@ -164,40 +166,40 @@
         ).wait_recv()
 
     for k in range(3):
-        remote(e_own, e1.at[k], ss.at[0], ve.at[0], line[k][1])
+        remote(e_own, e1.at[k], ss.at[1], ve.at[0], line[k][1])
     for c, (a, b) in enumerate(CHUNKS):
         for n in range(a, b):
-            for k in range(3):
+            for k in line_order if n % 2 == 0 else square_order:
                 if n % 2 == 0:
                     place, peer = line[k]
                     piece = pk.at[n, place]
                 else:
                     place, peer = square[k]
                     piece = pk.at[n, :, place]
-                remote(piece, r1.at[n, k], ss.at[1], v1.at[c], peer)
+                remote(piece, r1.at[n, k], ss.at[0], v1.at[c], peer)
     arrived(e1, ve.at[0])
     extra = e_own[...] + e1[0] + e1[1] + e1[2]
     e_line[...] = extra
     for k in range(3):
-        remote(e_line, e2.at[k], ss.at[0], ve.at[1], square[k][1])
+        remote(e_line, e2.at[k], ss.at[1], ve.at[1], square[k][1])
     for c, (a, b) in enumerate(CHUNKS):
         with jax.named_scope("one_%d" % c):
             arrived(r1.at[a:b], v1.at[c])
         for n in range(a, b):
             own = pk[n, xx] if n % 2 == 0 else pk[n, :, w]
             s1[n] = own + r1[n, 0] + r1[n, 1] + r1[n, 2]
-            for k in range(3):
+            for k in square_order if n % 2 == 0 else line_order:
                 place, peer = square[k] if n % 2 == 0 else line[k]
-                remote(s1.at[n, place], r2.at[n, k], ss.at[2], v2.at[c], peer)
+                remote(s1.at[n, place], r2.at[n, k], ss.at[0], v2.at[c], peer)
     arrived(e2, ve.at[1])
     extra = e_line[...] + e2[0] + e2[1] + e2[2]
     e_near[...] = extra
-    remote(e_near, e3.at[0], ss.at[7], ve.at[2], partner)
+    remote(e_near, e3.at[0], ss.at[1], ve.at[2], partner)
 
     @pl.when(late == 1)
     def _():
-        remote(e_near, e3.at[1], ss.at[7], ve.at[3], across)
-        remote(e_near, e3.at[2], ss.at[7], ve.at[3], opposite)
+        remote(e_near, e3.at[1], ss.at[1], ve.at[3], across)
+        remote(e_near, e3.at[2], ss.at[1], ve.at[3], opposite)
 
     for c, (a, b) in enumerate(CHUNKS):
         with jax.named_scope("two_%d" % c):
@@ -206,22 +208,22 @@
             own = s1[n, w] if n % 2 == 0 else s1[n, xx]
             s2[n] = own + r2[n, 0] + r2[n, 1] + r2[n, 2]
         mine = s2.at[a:b]
-        remote(mine, r3.at[0, a:b], ss.at[3], v3.at[c], partner)
+        remote(mine, r3.at[0, a:b], ss.at[0], v3.at[c], partner)
 
         @pl.when(late == 1)
         def _():
-            remote(mine, r3.at[1, a:b], ss.at[3], v5.at[c], across)
-            remote(mine, r3.at[2, a:b], ss.at[3], v5.at[c], opposite)
+            remote(mine, r3.at[1, a:b], ss.at[0], v5.at[c], across)
+            remote(mine, r3.at[2, a:b], ss.at[0], v5.at[c], opposite)
 
     @pl.when(late == 0)
     def _():
         arrived(e3.at[0], ve.at[2])
         e_two[...] = e_near[...] + e3[0]
-        remote(e_two, e3.at[1], ss.at[7], ve.at[3], across)
+        remote(e_two, e3.at[1], ss.at[1], ve.at[3], across)
         for c, (a, b) in enumerate(CHUNKS):
             arrived(r3.at[0, a:b], v3.at[c])
             s3[a:b] = s2[a:b] + r3[0, a:b]
-            remote(s3.at[a:b], r3.at[1, a:b], ss.at[3], v5.at[c], across)
+            remote(s3.at[a:b], r3.at[1, a:b], ss.at[0], v5.at[c], across)
 
     me = xx * 4 + w
     for c, (a, b) in enumerate(CHUNKS):
@@ -240,7 +242,7 @@
 
         for k in range(NEAR - 1):
             where = gf.at[a:b, me]
-            remote(where, where, ss.at[4], v4.at[c], near[k])
+            remote(where, where, ss.at[0], v4.at[c], near[k])
 
     @pl.when(late == 0)
     def _():
@@ -285,6 +287,7 @@
         if b == EARLY:
             for i, j in ((slice(0, half), slice(0, OUTPUTS)), (slice(half, OUTPUTS), slice(half, OUTPUTS))):
                 sq[i, j] = product((gh[i, :half], gl[i, :half]), (gh[:half, j], gl[:half, j]))
+            sq[:half, :half] += product((gh[:half, half:], gl[:half, half:]), (gh[half:, :half], gl[half:, :half]))
     divisor = jnp.sqrt(trace) + norm_floor
     inverse = 1.0 / (divisor * divisor)
     factor = (update_gain * math.sqrt(max(FEATURES, OUTPUTS))) / divisor
@@ -324,7 +327,9 @@
             return sum(product(rows[k], (pair[0][both[k], j], pair[1][both[k], j])) for k in order)
 
         for i, j in spots:
-            square = sq[i, j] + product((gh[i, half:], gl[i, half:]), (gh[half:, j], gl[half:, j]))
+            square = sq[i, j]
+            if j is far_half:
+                square = square + product((gh[i, half:], gl[i, half:]), (gh[half:, j], gl[half:, j]))
             value = (cubic_term * inverse) * g_ref[i, j] + (
                 quintic_term * inverse * inverse
             ) * square
@@ -361,11 +366,11 @@
 
     def send(matrix, first, last, sem, peer):
         where = part(matrix, first, last)
-        remote(where, where, ss.at[5], sem, peer)
+        remote(where, where, ss.at[2], sem, peer)
 
     def send_mate(matrix, first, last):
         where = part(matrix, first, last)
-        remote(where, where, ss.at[6], vm.at[0], mate)
+        remote(where, where, ss.at[3], vm.at[0], mate)
 
     def left_all(ref, sem):
         pltpu.make_async_remote_copy(
@@ -381,23 +386,28 @@
     def send_own(parts, sems):
         for i in range(parts):
             first, second = rows_of(i, parts)
-            send(dp, *first, sems.at[i], right)
-            send(dp, *second, sems.at[i], left)
+            sem = sems.at[min(i, parts // 2)]
+            send(dp, *first, sem, right)
+            send(dp, *second, sem, left)
         send_mate(dp, 0, B)
 
-    def from_near(i, parts, sems, c, onward):
+    def from_near(i, parts, sems, c):
         first, second = rows_of(i, parts)
         m_left, m_right = h_left * 2 + c, h_right * 2 + c
         arrived(part(0, 0, 2 * B // parts), sems.at[i])
-        if onward:
-            send(m_left, *first, sems.at[parts + i], right)
-            send(m_right, *second, sems.at[parts + i], left)
+        send(m_left, *first, sems.at[parts // 2 + 1 + i], right)
+        send(m_right, *second, sems.at[parts // 2 + 1 + i], left)
         send_mate(m_left, *first)
         send_mate(m_right, *second)
 
+    def the_rest(parts, sems, c):
+        arrived(part(0, 0, B), sems.at[parts // 2])
+        send_mate(h_left * 2 + c, B // 2, B)
+        send_mate(h_right * 2 + c, 0, B // 2)
+
     def from_far(i, parts, sems, c):
         first, second = rows_of(i, parts)
-        arrived(part(0, 0, 2 * B // parts), sems.at[parts + i])
+        arrived(part(0, 0, 2 * B // parts), sems.at[parts // 2 + 1 + i])
         send_mate(h_far * 2 + c, *first)
         send_mate(h_far * 2 + c, *second)
 
@@ -406,51 +416,40 @@
         send_own(PARTS0, vu0)
         with jax.named_scope("u_mate0"):
             arrived(o_ref.at[0:7], vm.at[0])
-        left_all(o_ref.at[0:2], ss.at[5])
-        left_all(o_ref.at[0:1], ss.at[6])
+        left_all(o_ref.at[0:2], ss.at[2])
+        left_all(o_ref.at[0:1], ss.at[3])
 
     @pl.when(core == 1)
     def _():
         send_own(PARTS1, vu1)
         with jax.named_scope("n_near1"):
             for i in range(PARTS1 // 2):
-                from_near(i, PARTS1, vu1, 1, True)
+                from_near(i, PARTS1, vu1, 1)
         with jax.named_scope("n_rest1"):
-            for i in range(PARTS1 // 2, PARTS1):
-                from_near(i, PARTS1, vu1, 1, False)
+            the_rest(PARTS1, vu1, 1)
         with jax.named_scope("n_near0"):
             for i in range(PARTS0 // 2):
-                from_near(i, PARTS0, vu0, 0, True)
+                from_near(i, PARTS0, vu0, 0)
         with jax.named_scope("n_far1"):
             for i in range(PARTS1 // 2):
                 from_far(i, PARTS1, vu1, 1)
         with jax.named_scope("n_rest0"):
-            for i in range(PARTS0 // 2, PARTS0):
-                from_near(i, PARTS0, vu0, 0, False)
+            the_rest(PARTS0, vu0, 0)
         with jax.named_scope("n_far0"):
             for i in range(PARTS0 // 2):
                 from_far(i, PARTS0, vu0, 0)
         with jax.named_scope("n_mate"):
             arrived(o_ref.at[0:1], vm.at[0])
-            left_all(o_ref.at[0:4], ss.at[5])
-            left_all(o_ref.at[0:7], ss.at[6])
+            left_all(o_ref.at[0:4], ss.at[2])
+            left_all(o_ref.at[0:7], ss.at[3])
 
     with jax.named_scope("drain"):
-        left_all(e_all.at[0:2], ss.at[0])
-        left_all(r1, ss.at[1])
-        left_all(r2, ss.at[2])
-
-        @pl.when(late == 0)
-        def _():
-            left_all(r3.at[0:2], ss.at[3])
-            left_all(e3.at[0:2], ss.at[7])
-
-        @pl.when(late == 1)
-        def _():
-            left_all(r3, ss.at[3])
-            left_all(e3, ss.at[7])
-
-        left_all(gf.at[:, 0:NEAR - 1], ss.at[4])
+        for count in range(2):
+
+            @pl.when(late == count)
+            def _():
+                left_all(sized.at[0:256 + 8 * count], ss.at[0])
+                left_all(e_sized.at[0:8 + count], ss.at[1])
 
 
 def on_device(gradient):
@@ -477,10 +476,12 @@
             pltpu.VMEM((OUTPUTS, OUTPUTS), bf16),
             pltpu.VMEM((OUTPUTS, OUTPUTS), f32),
             *[pltpu.VMEM((OUTPUTS, OUTPUTS), bf16) for _ in range(10)],
+            pltpu.VMEM((264, TILE, B), f32),
+            pltpu.VMEM((9, 2, B), f32),
             dma,
-            dma((8,)),
+            dma((4,)),
             *[dma((len(CHUNKS),)) for _ in range(5)],
-            dma((4,)), dma((PARTS0 * 3 // 2,)), dma((PARTS1 * 3 // 2,)), dma((1,)),
+            dma((4,)), dma((PARTS0 + 1,)), dma((PARTS1 + 1,)), dma((1,)),
         ],
         compiler_params=pltpu.CompilerParams(
             collective_id=0, has_side_effects=True, vmem_limit_bytes=VMEM_LIMIT

time: 48.4 us -> 48.4 us (level)
  no operation moved by 1% of the time
where the time goes in v7:
time: 48.4 us; the launch traced here: 48.2 us
  Pallas kernels  47.3 us (98%)
  local copies, waits for them, and re-layouts  0.97 us (2%)
    pallas_call x1, Pallas kernels, on_device(): pl.pallas_call(kernel, out_shape=pltpu.VMEM((8, B, OUTPUTS), bf16), in_sp...  47.3 us
    unnamed x1, local copies, waits for them, and re-layouts  0.97 us

profile of v7, /device:TPU:1, one launch (start us, length us, event | category | flops | bytes accessed | tf_op | source)
XLA Modules:
  0.0 48.2 jit_solution(8369892286321865250)
XLA Ops:
  0.0 47.3 %gram_step.1 = bf16[8,128,512]{2,1,0:T(8,128)(2,1)S(1)} custom-call(f32[1,128,512]{2,1,0:T(8,128)} %x_hbm.1), custom_call_target="tpu_custom_call" | custom-call | tf_op jit(solution)/shard_map/gram_step/pallas_call | solution.py:457
  47.3 1.0 %copy.3 = bf16[8,128,512]{2,1,0:T(8,128)(2,1)} copy(bf16[8,128,512]{2,1,0:T(8,128)(2,1)S(1)} %gram_step.1) | data formatting | bytes 2097152

commit v8 on v7

--- a/solution.py
+++ b/solution.py
@@ -425,16 +425,16 @@
         with jax.named_scope("n_near1"):
             for i in range(PARTS1 // 2):
                 from_near(i, PARTS1, vu1, 1)
-        with jax.named_scope("n_rest1"):
-            the_rest(PARTS1, vu1, 1)
         with jax.named_scope("n_near0"):
             for i in range(PARTS0 // 2):
                 from_near(i, PARTS0, vu0, 0)
+        with jax.named_scope("n_rest1"):
+            the_rest(PARTS1, vu1, 1)
+        with jax.named_scope("n_rest0"):
+            the_rest(PARTS0, vu0, 0)
         with jax.named_scope("n_far1"):
             for i in range(PARTS1 // 2):
                 from_far(i, PARTS1, vu1, 1)
-        with jax.named_scope("n_rest0"):
-            the_rest(PARTS0, vu0, 0)
         with jax.named_scope("n_far0"):
             for i in range(PARTS0 // 2):
                 from_far(i, PARTS0, vu0, 0)

time: 48.4 us -> 48.4 us (level)
  no operation moved by 1% of the time
where the time goes in v8:
time: 48.4 us; the launch traced here: 48.2 us
  Pallas kernels  47.3 us (98%)
  local copies, waits for them, and re-layouts  0.97 us (2%)
    pallas_call x1, Pallas kernels, on_device(): pl.pallas_call(kernel, out_shape=pltpu.VMEM((8, B, OUTPUTS), bf16), in_sp...  47.3 us
    unnamed x1, local copies, waits for them, and re-layouts  0.97 us

profile of v8, /device:TPU:1, one launch (start us, length us, event | category | flops | bytes accessed | tf_op | source)
XLA Modules:
  0.0 48.2 jit_solution(1366264360714224520)
XLA Ops:
  0.0 47.3 %gram_step.1 = bf16[8,128,512]{2,1,0:T(8,128)(2,1)S(1)} custom-call(f32[1,128,512]{2,1,0:T(8,128)} %x_hbm.1), custom_call_target="tpu_custom_call" | custom-call | tf_op jit(solution)/shard_map/gram_step/pallas_call | solution.py:457
  47.3 1.0 %copy.3 = bf16[8,128,512]{2,1,0:T(8,128)(2,1)} copy(bf16[8,128,512]{2,1,0:T(8,128)(2,1)S(1)} %gram_step.1) | data formatting | bytes 2097152

commit v9 on v8

--- a/solution.py
+++ b/solution.py
@@ -397,13 +397,15 @@
         arrived(part(0, 0, 2 * B // parts), sems.at[i])
         send(m_left, *first, sems.at[parts // 2 + 1 + i], right)
         send(m_right, *second, sems.at[parts // 2 + 1 + i], left)
-        send_mate(m_left, *first)
-        send_mate(m_right, *second)
+        if c == 0:
+            send_mate(m_left, *first)
+            send_mate(m_right, *second)
 
     def the_rest(parts, sems, c):
         arrived(part(0, 0, B), sems.at[parts // 2])
-        send_mate(h_left * 2 + c, B // 2, B)
-        send_mate(h_right * 2 + c, 0, B // 2)
+        whole = c == 1
+        send_mate(h_left * 2 + c, 0 if whole else B // 2, B)
+        send_mate(h_right * 2 + c, 0, B if whole else B // 2)
 
     def from_far(i, parts, sems, c):
         first, second = rows_of(i, parts)

time: 48.4 us -> 48.4 us (level)
  no operation moved by 1% of the time
where the time goes in v9:
time: 48.4 us; the launch traced here: 48.2 us
  Pallas kernels  47.3 us (98%)
  local copies, waits for them, and re-layouts  0.97 us (2%)
    pallas_call x1, Pallas kernels, on_device(): pl.pallas_call(kernel, out_shape=pltpu.VMEM((8, B, OUTPUTS), bf16), in_sp...  47.3 us
    unnamed x1, local copies, waits for them, and re-layouts  0.97 us

profile of v9, /device:TPU:1, one launch (start us, length us, event | category | flops | bytes accessed | tf_op | source)
XLA Modules:
  0.0 48.2 jit_solution(5699804763248035493)
XLA Ops:
  0.0 47.3 %gram_step.1 = bf16[8,128,512]{2,1,0:T(8,128)(2,1)S(1)} custom-call(f32[1,128,512]{2,1,0:T(8,128)} %x_hbm.1), custom_call_target="tpu_custom_call" | custom-call | tf_op jit(solution)/shard_map/gram_step/pallas_call | solution.py:459
  47.3 1.0 %copy.3 = bf16[8,128,512]{2,1,0:T(8,128)(2,1)} copy(bf16[8,128,512]{2,1,0:T(8,128)(2,1)S(1)} %gram_step.1) | data formatting | bytes 2097152
